TPU v7x, 32 devices: a whole 2x2x4 slice. The times are simulated.
32 devices in a mesh: seq: 4 (over z), tensor: 2 (over x), dp: 4 (over y, core).
Axes of the slice: x: 2, y: 2, z: 4, core: 2. Of those that a mesh axis runs over, the one named last changes fastest.
Arguments:
- tokens: bfloat16 [4, 1024, 3072], P('dp', 'seq'), may hold values from -6 to 6
- cotangent: bfloat16 [4, 1024, 3072], P('dp', 'seq'), may hold values from -6 to 6
- qkv_weight: bfloat16 [3072, 3, 768], P(('seq', 'dp'), None, 'tensor'), may hold values from -0.109375 to 0.109375
- out_weight: bfloat16 [3072, 768], P(('seq', 'dp'), 'tensor'), may hold values from -0.21875 to 0.21875
Outputs:
- qkv_grad: float32 [3072, 3, 768], P(('seq', 'dp'), None, 'tensor')
- out_grad: float32 [3072, 768], P(('seq', 'dp'), 'tensor')
- branch_grad: bfloat16 [4, 1024, 3072], P('dp', 'seq', 'tensor')
All inputs are finite; a program needn't handle non-finite values.
Results may differ from a plain program's by a relative error of at most 0.025.
Values may be sent and summed in bfloat16 or wider, within the bound.
A program may use at most 128 MiB of HBM per device.

v0:
```python
import functools

import jax
import jax.numpy as jnp
from jax import lax
from jax.experimental import pallas as pl
from jax.experimental.pallas import tpu as pltpu
from jax.sharding import PartitionSpec as P

HD = 128

CORES = 2
CHUNKS = 2
MESH_ID = pl.DeviceIdType.MESH


def greet(seq_count, chip_count, place, chip, core):
    barrier = pltpu.get_barrier_semaphore()

    def signal(device):
        pl.semaphore_signal(barrier, inc=1, device_id=device, device_id_type=MESH_ID)

    @pl.when(place > 0)
    def _():
        signal({"seq": place - 1})

    @pl.when(place < seq_count - 1)
    def _():
        signal({"seq": place + 1})

    for step in range(1, chip_count):
        signal({"dp": (chip + step) % chip_count * CORES + core})
    signal({"dp": chip * CORES + 1 - core})
    ends = jnp.minimum(place, 1) + jnp.minimum(seq_count - 1 - place, 1)
    pl.semaphore_wait(barrier, chip_count + ends)


def gather_kernel(
    seq_count, dp_count, own_ref, out_ref, recv, right_sem, left_sem, chip_sem, core_sem, own_sem
):
    chip_count = dp_count // CORES
    place = lax.axis_index("seq")
    index = lax.axis_index("dp")
    chip, core = index // CORES, index % CORES
    greet(seq_count, chip_count, place, chip, core)
    own_copy = pltpu.make_async_copy(own_ref, out_ref.at[place * dp_count + index], own_sem)
    own_copy.start()

    def copy(source, slot, send_sem, device):
        return pltpu.make_async_remote_copy(
            src_ref=source,
            dst_ref=out_ref.at[slot],
            send_sem=send_sem,
            recv_sem=recv.at[slot],
            device_id=device,
            device_id_type=MESH_ID,
        )

    def right(source, origin):
        return copy(
            source, origin * dp_count + index, right_sem.at[origin], {"seq": place + 1}
        )

    def left(source, origin):
        return copy(source, origin * dp_count + index, left_sem.at[origin], {"seq": place - 1})

    def across(source, origin, step):
        return copy(
            source,
            origin * dp_count + index,
            chip_sem.at[origin * chip_count + step],
            {"dp": (chip + step) % chip_count * CORES + core},
        )

    def beside(source, origin, source_chip):
        return copy(
            source,
            origin * dp_count + source_chip * CORES + core,
            core_sem.at[origin * chip_count + source_chip],
            {"dp": chip * CORES + 1 - core},
        )

    def landed(slot):
        copy(own_ref, slot, core_sem.at[0], {"dp": chip * CORES + 1 - core}).wait_recv()

    def spread(source, origin):
        for step in range(1, chip_count):
            across(source, origin, step).start()
        beside(source, origin, chip).start()

    @pl.when(place < seq_count - 1)
    def _():
        right(own_ref, place).start()

    @pl.when(place > 0)
    def _():
        left(own_ref, place).start()

    spread(own_ref, place)
    for step in range(1, seq_count):
        low, high = place - step, place + step

        @pl.when(low >= 0)
        def _():
            slot = low * dp_count + index
            landed(slot)

            @pl.when(place < seq_count - 1)
            def _():
                right(out_ref.at[slot], low).start()

            spread(out_ref.at[slot], low)

        @pl.when(high < seq_count)
        def _():
            slot = high * dp_count + index
            landed(slot)

            @pl.when(place > 0)
            def _():
                left(out_ref.at[slot], high).start()

            spread(out_ref.at[slot], high)

    for turn in range(seq_count):
        origin = (place + turn) % seq_count
        for step in range(1, chip_count):
            source_chip = (chip + step) % chip_count
            slot = origin * dp_count + source_chip * CORES + core
            landed(slot)
            beside(out_ref.at[slot], origin, source_chip).start()
    for origin in range(seq_count):
        for source_chip in range(chip_count):
            landed(origin * dp_count + source_chip * CORES + 1 - core)
    own_copy.wait()
    for origin in range(seq_count):
        for step in range(1, chip_count):
            across(own_ref, origin, step).wait_send()
        for source_chip in range(chip_count):
            beside(own_ref, origin, source_chip).wait_send()

        @pl.when((origin <= place) & (place < seq_count - 1))
        def _():
            right(own_ref, origin).wait_send()

        @pl.when((origin >= place) & (place > 0))
        def _():
            left(own_ref, origin).wait_send()


def gather_rows(own):
    seq_count, dp_count = lax.axis_size("seq"), lax.axis_size("dp")
    chip_count = dp_count // CORES
    return pl.pallas_call(
        functools.partial(gather_kernel, seq_count, dp_count),
        out_shape=jax.ShapeDtypeStruct((seq_count * dp_count,) + own.shape, own.dtype),
        in_specs=[pl.BlockSpec(memory_space=pltpu.VMEM)],
        out_specs=pl.BlockSpec(memory_space=pl.ANY),
        scratch_shapes=[
            pltpu.SemaphoreType.DMA((seq_count * dp_count,)),
            pltpu.SemaphoreType.DMA((seq_count,)),
            pltpu.SemaphoreType.DMA((seq_count,)),
            pltpu.SemaphoreType.DMA((seq_count * chip_count,)),
            pltpu.SemaphoreType.DMA((seq_count * chip_count,)),
            pltpu.SemaphoreType.DMA,
        ],
        compiler_params=pltpu.CompilerParams(collective_id=0, has_side_effects=True),
        cost_estimate=pl.CostEstimate(flops=0, bytes_accessed=150000000, transcendentals=0),
        name="gather_rows",
    )(own)

def scatter_kernel(
    seq_count,
    dp_count,
    term_ref,
    out_ref,
    held,
    chip_in,
    low_in,
    high_in,
    core_recv,
    core_send,
    chip_recv,
    chip_send,
    low_recv,
    high_recv,
    chain_send,
):
    chip_count = dp_count // CORES
    part_rows = term_ref.shape[1] // CHUNKS
    place = lax.axis_index("seq")
    index = lax.axis_index("dp")
    chip, core = index // CORES, index % CORES
    greet(seq_count, chip_count, place, chip, core)

    def piece(ref, slot, part):
        return ref.at[slot, pl.ds(part * part_rows, part_rows)]

    def copy(source, target_ref, part, slot, send_sem, recv_sem, device):
        return pltpu.make_async_remote_copy(
            src_ref=source,
            dst_ref=piece(target_ref, slot, part),
            send_sem=send_sem.at[slot * CHUNKS + part],
            recv_sem=recv_sem.at[slot * CHUNKS + part],
            device_id=device,
            device_id_type=MESH_ID,
        )

    def beside(part, target, target_chip):
        source = piece(term_ref, target * dp_count + target_chip * CORES + 1 - core, part)
        slot = target * chip_count + target_chip
        device = {"dp": chip * CORES + 1 - core}
        return copy(source, held, part, slot, core_send, core_recv, device)

    def across(part, target, step):
        other = (chip + step) % chip_count
        source = piece(held, target * chip_count + other, part)
        slot = (step - 1) * seq_count + target
        device = {"dp": other * CORES + core}
        return copy(source, chip_in, part, slot, chip_send, chip_recv, device)

    def upward(part, target):
        source = piece(held, target * chip_count + chip, part)
        return copy(source, low_in, part, target, chain_send, low_recv, {"seq": place + 1})

    def downward(part, target):
        source = piece(held, target * chip_count + chip, part)
        return copy(source, high_in, part, target, chain_send, high_recv, {"seq": place - 1})

    def add(slot, part, others):
        @pl.loop(0, part_rows // 16)
        def _(step):
            rows = pl.ds(pl.multiple_of(part * part_rows + step * 16, 16), 16)
            total = held[slot, rows, :].astype(jnp.float32)
            for ref, other in others:
                total = total + ref[other, rows, :].astype(jnp.float32)
            held[slot, rows, :] = total.astype(held.dtype)

    order = []
    for turn in range((seq_count + 1) // 2):
        order.extend(sorted({seq_count - 1 - turn, turn}, reverse=True))
    items = [(part, target) for part in range(CHUNKS) for target in order]
    for part, target in items:
        for step in range(1, chip_count):
            beside(part, target, (chip + step) % chip_count).start()
    for part, target in items:
        beside(part, target, chip).start()
    for part, target in items:
        for step in range(1, chip_count):
            other = (chip + step) % chip_count
            beside(part, target, other).wait_recv()
            own_slot = target * dp_count + other * CORES + core
            add(target * chip_count + other, part, [(term_ref, own_slot)])
            across(part, target, step).start()
    for part, target in items:
        slot = target * chip_count + chip
        others = [(term_ref, target * dp_count + index)]
        beside(part, target, chip).wait_recv()
        for step in range(1, chip_count):
            across(part, target, step).wait_recv()
            others.append((chip_in, (step - 1) * seq_count + target))
        add(slot, part, others)
        if target > 0:

            @pl.when(place < target)
            def _():
                @pl.when(place > 0)
                def _():
                    upward(part, target).wait_recv()
                    add(slot, part, [(low_in, target)])

                upward(part, target).start()

        if target < seq_count - 1:

            @pl.when(place > target)
            def _():
                @pl.when(place < seq_count - 1)
                def _():
                    downward(part, target).wait_recv()
                    add(slot, part, [(high_in, target)])

                downward(part, target).start()

    out_ref[...] = held[place * chip_count + chip].astype(jnp.float32)

    @pl.when(place > 0)
    def _():
        for part in range(CHUNKS):
            upward(part, place).wait_recv()
        out_ref[...] += low_in[place].astype(jnp.float32)

    @pl.when(place < seq_count - 1)
    def _():
        for part in range(CHUNKS):
            downward(part, place).wait_recv()
        out_ref[...] += high_in[place].astype(jnp.float32)

    for part, target in items:
        for step in range(1, chip_count):
            across(part, target, step).wait_send()
        for target_chip in range(chip_count):
            beside(part, target, target_chip).wait_send()

        @pl.when(place != target)
        def _():
            upward(part, target).wait_send()


def scatter_rows(terms):
    seq_count, dp_count = lax.axis_size("seq"), lax.axis_size("dp")
    chip_count = dp_count // CORES
    shape = terms.shape[1:]

    def slots(count):
        return pltpu.VMEM((count,) + shape, terms.dtype)

    def semaphores(count):
        return pltpu.SemaphoreType.DMA((count * CHUNKS,))

    both, peers = seq_count * chip_count, seq_count * (chip_count - 1)
    return pl.pallas_call(
        functools.partial(scatter_kernel, seq_count, dp_count),
        out_shape=jax.ShapeDtypeStruct(shape, jnp.float32),
        in_specs=[pl.BlockSpec(memory_space=pltpu.VMEM)],
        out_specs=pl.BlockSpec(memory_space=pltpu.VMEM),
        scratch_shapes=[
            slots(both),
            slots(peers),
            slots(seq_count),
            slots(seq_count),
            semaphores(both),
            semaphores(both),
            semaphores(peers),
            semaphores(peers),
            semaphores(seq_count),
            semaphores(seq_count),
            semaphores(seq_count),
        ],
        compiler_params=pltpu.CompilerParams(
            collective_id=1, has_side_effects=True, vmem_limit_bytes=40 * 1024 * 1024
        ),
        cost_estimate=pl.CostEstimate(flops=0, bytes_accessed=180000000, transcendentals=0),
        name="scatter_rows",
    )(terms)


epsilon = 1e-06


def normalize(values):
    average = jnp.mean(values, axis=-1, keepdims=True)
    centered = values - average
    inverse = lax.rsqrt(jnp.mean(centered * centered, axis=-1, keepdims=True) + epsilon)
    return (centered * inverse, inverse)


def normalize_back(gradient, normed, inverse):
    mean_grad = jnp.mean(gradient, axis=-1, keepdims=True)
    mean_both = jnp.mean(gradient * normed, axis=-1, keepdims=True)
    return (gradient - mean_grad - normed * mean_both) * inverse


def local(tokens, cotangent, qkv_weight, out_weight):
    row_count = tokens.shape[1]
    feature_count = tokens.shape[2]
    column_count = out_weight.shape[1]
    head_count = column_count // HD
    score_scale = HD ** (-0.5)
    own_rows = qkv_weight.shape[0]
    grad_rows = cotangent[0]
    normed, inverse = normalize(tokens[0].astype(jnp.float32))
    unit_low = normed.astype(jnp.bfloat16)
    flat_weight = qkv_weight.reshape(own_rows, 3 * column_count)
    piece_all = gather_rows(jnp.concatenate([flat_weight, out_weight], axis=1)).reshape(
        feature_count, 4 * column_count
    )
    piece_qkv = piece_all[:, : 3 * column_count]
    piece_out = piece_all[:, 3 * column_count :]
    piece_rows = piece_qkv.shape[0]
    left_rows = unit_low
    right_rows = grad_rows
    projected = jnp.dot(left_rows, piece_qkv, preferred_element_type=jnp.float32)
    attended_grad = jnp.dot(right_rows, piece_out, preferred_element_type=jnp.float32)
    full_qkv = piece_qkv
    projected, attended_grad, full_qkv = (projected, attended_grad, full_qkv)
    query_unit, query_inv = normalize(
        projected[:, :column_count].reshape(row_count, head_count, HD)
    )
    key_unit, key_inv = normalize(
        projected[:, column_count : 2 * column_count].reshape(row_count, head_count, HD)
    )
    query_low = query_unit.astype(jnp.bfloat16)
    key_value = jnp.stack(
        [
            key_unit.astype(jnp.bfloat16).reshape(row_count, column_count),
            projected[:, 2 * column_count :].astype(jnp.bfloat16),
        ]
    )
    grad_low = attended_grad.astype(jnp.bfloat16).reshape(row_count, head_count, HD)

    def scores_of(key_rows):
        piece_rows = key_rows.shape[0]
        return (
            jnp.einsum(
                "qhd,khd->hqk",
                query_low,
                key_rows.reshape(piece_rows, head_count, HD),
                preferred_element_type=jnp.float32,
            )
            * score_scale
        )

    every_pair = lax.all_gather(key_value, "seq", axis=1, tiled=True)
    piece_rows = every_pair.shape[1]
    exponent = jnp.exp(scores_of(every_pair[0]))
    add_exp_total = jnp.sum(exponent, axis=-1)
    weighted = jnp.einsum(
        "hqk,khd->qhd",
        exponent.astype(jnp.bfloat16),
        every_pair[1].reshape(piece_rows, head_count, HD),
        preferred_element_type=jnp.float32,
    )
    exp_total, weighted = (add_exp_total, weighted)
    attended_low = (weighted / exp_total.T[:, :, None]).astype(jnp.bfloat16)
    row_delta = jnp.sum(grad_low.astype(jnp.float32) * attended_low.astype(jnp.float32), axis=-1)
    piece_rows = every_pair.shape[1]
    key_rows = every_pair[0].reshape(piece_rows, head_count, HD)
    value_rows = every_pair[1].reshape(piece_rows, head_count, HD)
    probability = jnp.exp(scores_of(every_pair[0])) / exp_total[:, :, None]
    prob_grad = jnp.einsum("qhd,khd->hqk", grad_low, value_rows, preferred_element_type=jnp.float32)
    grad_score = (probability * (prob_grad - row_delta.T[:, :, None]) * score_scale).astype(
        jnp.bfloat16
    )
    query_part = jnp.einsum(
        "hqk,khd->qhd", grad_score, key_rows, preferred_element_type=jnp.float32
    )
    key_part = jnp.einsum("hqk,qhd->khd", grad_score, query_low, preferred_element_type=jnp.float32)
    value_part = jnp.einsum(
        "hqk,qhd->khd",
        probability.astype(jnp.bfloat16),
        grad_low,
        preferred_element_type=jnp.float32,
    )
    every_grad = jnp.stack(
        [key_part.reshape(piece_rows, column_count), value_part.reshape(piece_rows, column_count)]
    )
    pair_grad = lax.psum_scatter(
        every_grad.astype(jnp.bfloat16), "seq", scatter_dimension=1, tiled=True
    ).astype(jnp.float32)
    query_back = normalize_back(query_part, query_unit, query_inv)
    key_back = normalize_back(pair_grad[0].reshape(row_count, head_count, HD), key_unit, key_inv)
    qkv_low = jnp.concatenate(
        [
            query_back.reshape(row_count, column_count),
            key_back.reshape(row_count, column_count),
            pair_grad[1],
        ],
        axis=1,
    ).astype(jnp.bfloat16)
    inner_grad = jnp.einsum("rc,dc->rd", qkv_low, full_qkv, preferred_element_type=jnp.float32)
    attended_flat = attended_low.reshape(row_count, column_count)
    share_width = feature_count // lax.axis_size("tensor")
    tensor_count, tensor_at = lax.axis_size("tensor"), lax.axis_index("tensor")

    def share_of(values, owner):
        return lax.dynamic_slice_in_dim(values, owner * share_width, share_width, 1)

    def shifted(values, step):
        pairs = [(place, (place + step) % tensor_count) for place in range(tensor_count)]
        return lax.ppermute(values, "tensor", pairs)

    inner_low = inner_grad.astype(jnp.bfloat16)
    arrived = [
        shifted(share_of(inner_low, (tensor_at + step) % tensor_count), step)
        for step in range(1, tensor_count)
    ]
    left_rows = unit_low
    right_rows = grad_rows
    qkv_term = jnp.einsum(
        "rd,rc->dc", left_rows, qkv_low, preferred_element_type=jnp.float32
    ).astype(jnp.bfloat16)
    out_term = jnp.einsum(
        "rd,rc->dc", right_rows, attended_flat, preferred_element_type=jnp.float32
    ).astype(jnp.bfloat16)
    terms = jnp.concatenate([qkv_term, out_term], axis=1)
    terms = terms.reshape(-1, own_rows, 4 * column_count)
    arrived, terms = lax.optimization_barrier((arrived, terms))
    share = share_of(inner_low, tensor_at).astype(jnp.float32)
    for other in arrived:
        share = share + other.astype(jnp.float32)
    unit_share = share_of(normed, tensor_at)
    own_sums = jnp.stack([jnp.sum(share, axis=-1), jnp.sum(share * unit_share, axis=-1)])
    both_sums = own_sums
    for step in range(1, tensor_count):
        both_sums = both_sums + shifted(own_sums, step)
    means = both_sums[:, :, None] / feature_count
    branch = (share - means[0] - unit_share * means[1]) * inverse
    summed = scatter_rows(terms)
    return (
        summed[:, : 3 * column_count].reshape(own_rows, 3, column_count),
        summed[:, 3 * column_count :],
        branch.astype(jnp.bfloat16)[None],
    )


def solution(mesh):
    return jax.shard_map(
        local,
        mesh=mesh,
        in_specs=(
            P("dp", "seq", None),
            P("dp", "seq", None),
            P(("seq", "dp"), None, "tensor"),
            P(("seq", "dp"), "tensor"),
        ),
        out_specs=(
            P(("seq", "dp"), None, "tensor"),
            P(("seq", "dp"), "tensor"),
            P("dp", "seq", "tensor"),
        ),
        check_vma=False,
    )
```

profile of v0, /device:TPU:0, one launch (start us, length us, event | category | flops | bytes accessed | tf_op | source)
XLA Modules:
  0.0 309.0 jit_solution(13360908511394105224)
XLA Ops:
  8.4 1.8 pad_maximum_fusion.2.own_ref
  10.2 63.3 %gather_rows.1 = bf16[16,192,1536]{2,1,0:T(8,128)(2,1)} custom-call(bf16[192,1536]{1,0:T(8,128)(2,1)} %pad_maximum_fusion.2.own_ref), custom_call_target="tpu_custom_call" | custom-call | bytes 150000000 | tf_op jit(solution)/shard_map/gather_rows/pallas_call | solution.py:154
  74.4 5.3 %fusion.2 = f32[256,1152]{1,0:T(8,128)S(1)} fusion(bf16[3072,1536]{1,0:T(8,128)(2,1)} %bitcast.99, bf16[1,256,3072]{2,1,0:T(8,128)(2,1)S(1)} %copy-done.3, f32[256]{0:T(256)S(1)} %add_rsqrt_fusion.2, f32[256]{0:T(256)S(1)} %broadcast_multiply_fusion.6), kind=kOutput, calls=%fused_computation.4 | convolution fusion | flops 1815085056 | bytes 9832448 | tf_op jit(solution)/shard_map/dot_general | solution.py:383
  83.6 1.9 copy.27
  86.3 1.9 copy.26
  88.2 2.2 fusion.62
  90.4 1.7 pad_maximum_fusion.4
  93.7 3.2 %fusion.37 = bf16[384,256]{1,0:T(8,128)(2,1)} fusion(bf16[1,256,3072]{2,1,0:T(8,128)(2,1)S(1)} %copy-done, bf16[3072,1536]{1,0:T(8,128)(2,1)} %bitcast.100), kind=kOutput, calls=%fused_computation.39 | convolution fusion | flops 604078080 | bytes 4128768 | tf_op jit(solution)/shard_map/dot_general | solution.py:384
  96.9 31.0 %all-gather.2.cloned.1.call-done = bf16[2,1024,384]{2,1,0:T(8,128)(2,1)} async-done(((bf16[2,256,384]{2,1,0:T(8,128)(2,1)}), bf16[2,1024,384]{2,1,0:T(8,128)(2,1)}) %all-gather.2.cloned.1.call-update) | async-done | bytes 1572880 | tf_op jit(solution)/shard_map/all_gather | solution.py:414
  127.8 2.7 fusion.61
  130.5 2.3 copy.28
  132.8 2.0 fusion.14
  134.8 1.9 fusion.24
  136.7 2.3 copy.36
  139.0 2.3 copy.32
  141.3 3.6 %multiply_reduce_fusion.3 = (f32[256,3]{0,1:T(4,128)S(1)}, bf16[256,3,128]{0,2,1:T(8,128)(2,1)}) fusion(bf16[256,3,128]{0,2,1:T(8,128)(2,1)} %bitcast.129, f32[256,3]{0,1:T(4,128)} %bitcast.126, bf16[1024,3,128]{0,2,1:T(8,128)(2,1)} %bitcast.116, f32[3,256,1024]{2,1,0:T(8,128)} %copy-done.16), kind=kOutput, calls=%fused_computation.55 | convolution fusion | flops 203488512 | bytes 4331520 | tf_op jit(solution)/shard_map/hqk,khd->qhd/dot_general | solution.py:418
  148.5 2.3 copy.35
  150.8 2.8 pad_maximum_fusion.1
  153.7 3.1 %fusion.9 = f32[256,3072]{1,0:T(8,128)} fusion(bf16[1,256,3072]{2,1,0:T(8,128)(2,1)S(1)} %copy-done.3, f32[256]{0:T(256)} %copy-done.22, f32[256]{0:T(256)} %copy-done.24), kind=kLoop, calls=%fused_computation.12 | loop fusion | flops 2359296 | bytes 4720640 | tf_op jit(solution)/shard_map/mul | solution.py:355
  158.2 1.8 copy.41
  160.0 3.2 %fusion.4 = bf16[3072,384]{0,1:T(8,128)(2,1)} fusion(bf16[256,384]{0,1:T(8,128)(2,1)} %bitcast.121, bf16[1,256,3072]{2,1,0:T(8,128)(2,1)S(1)} %copy-done), kind=kOutput, calls=%fused_computation.9 | convolution fusion | flops 605159424 | bytes 4128768 | tf_op jit(solution)/shard_map/rd,rc->dc/dot_general | solution.py:483
  163.2 24.9 %reduce-scatter.2.cloned.1.call-done = bf16[2,256,384]{2,1,0:T(8,128)(2,1)} async-done(((bf16[2,1024,384]{2,1,0:T(8,128)(2,1)}), bf16[2,256,384]{2,1,0:T(8,128)(2,1)}) %reduce-scatter.2.cloned.1.call-update) | async-done | bytes 393232 | tf_op jit(solution)/shard_map/reduce_scatter | solution.py:448
  188.1 1.7 slice_convert_fusion.1
  191.9 5.3 %fusion.5 = bf16[256,3072]{1,0:T(8,128)(2,1)S(1)} fusion(bf16[3072,1536]{1,0:T(8,128)(2,1)} %bitcast.101, bf16[256,384]{1,0:T(8,128)(2,1)S(1)} %copy-done.21, bf16[256,384]{1,0:T(8,128)(2,1)S(1)} %fusion.48, bf16[256,384]{1,0:T(8,128)(2,1)S(1)} %copy-done.20), kind=kOutput, calls=%fused_computation.10 | convolution fusion | flops 1814495232 | bytes 9240576 | tf_op jit(solution)/shard_map/rc,dc->rd/dot_general | solution.py:461
  197.2 2.4 convolution_convert_fusion
  200.6 1.5 collective-permute-start
  202.0 9.9 %pad_maximum_fusion = bf16[3072,1536]{0,1:T(8,128)(2,1)} fusion(bf16[3072,384]{0,1:T(8,128)(2,1)S(1)} %copy-done.4, bf16[3072,1152]{0,1:T(8,128)(2,1)S(1)} %convolution_convert_fusion), kind=kLoop, calls=%fused_computation.1 | loop fusion | flops 18874368 | bytes 18874368 | tf_op jit(solution)/shard_map/concatenate | solution.py:486
  212.0 12.8 %copy.42 = bf16[3072,1536]{1,0:T(8,128)(2,1)} copy(bf16[3072,1536]{0,1:T(8,128)(2,1)} %pad_maximum_fusion) | data formatting | bytes 18874368 | tf_op jit(solution)/shard_map/concatenate | solution.py:486
  224.8 1.8 fusion.27
  227.2 3.7 %copy-done.2 = bf16[3072,1536]{1,0:T(8,128)(2,1)S(1)} copy-done((bf16[3072,1536]{1,0:T(8,128)(2,1)S(1)}, bf16[3072,1536]{1,0:T(8,128)(2,1)}, u32[]{:S(2)}) %copy-start.2) | copy-done | bytes 9437208
  230.9 66.5 %scatter_rows.1 = f32[192,1536]{1,0:T(8,128)S(1)} custom-call(bf16[16,192,1536]{2,1,0:T(8,128)(2,1)S(1)} %bitcast.92), custom_call_target="tpu_custom_call" | custom-call | bytes 180000000 | tf_op jit(solution)/shard_map/scatter_rows/pallas_call | solution.py:322
  299.7 2.4 fusion.43
  (105 shorter events, 19.1 us)
Async XLA Ops:
  7.2 86.5 %copy-start = (bf16[1,256,3072]{2,1,0:T(8,128)(2,1)S(1)}, bf16[1,256,3072]{2,1,0:T(8,128)(2,1)}, u32[]{:S(2)}) copy-start(bf16[1,256,3072]{2,1,0:T(8,128)(2,1)} %param.5) | copy-start | bytes 4718596
  7.2 120.7 %all-gather.2.cloned.1.call-start = ((), (), s32[]{:S(2)}) async-start(), calls=%async_computation.1 | async-start | bytes 1966080 | tf_op jit(solution)/shard_map/all_gather | solution.py:414
  10.2 63.3 %copy-start.3 = (bf16[1,256,3072]{2,1,0:T(8,128)(2,1)S(1)}, bf16[1,256,3072]{2,1,0:T(8,128)(2,1)}, u32[]{:S(2)}) copy-start(bf16[1,256,3072]{2,1,0:T(8,128)(2,1)} %param.4) | copy-start | bytes 4718596
  73.8 5.9 %copy-start.24 = (f32[256]{0:T(256)}, f32[256]{0:T(256)S(1)}, u32[]{:S(2)}) copy-start(f32[256]{0:T(256)S(1)} %broadcast_multiply_fusion.6) | copy-start | bytes 3076
  74.4 5.3 %copy-start.22 = (f32[256]{0:T(256)}, f32[256]{0:T(256)S(1)}, u32[]{:S(2)}) copy-start(f32[256]{0:T(256)S(1)} %add_rsqrt_fusion.2) | copy-start | bytes 3076
  82.7 7.7 %copy-start.8 = (f32[256,384]{0,1:T(8,128)}, f32[256,384]{0,1:T(8,128)S(1)}, u32[]{:S(2)}) copy-start(f32[256,384]{0,1:T(8,128)S(1)} %copy.25) | copy-start | bytes 1179652
  92.2 95.9 %reduce-scatter.2.cloned.1.call-start = ((), (), s32[]{:S(2)}) async-start(), calls=%async_computation.2 | async-start | bytes 1966080 | tf_op jit(solution)/shard_map/reduce_scatter | solution.py:448
  132.8 2.0 copy-start.28
  134.8 1.9 copy-start.16
  134.8 1.9 copy-start.26
  141.3 3.6 %copy-start.17 = (f32[3,256,1024]{2,1,0:T(8,128)S(1)}, f32[3,256,1024]{2,1,0:T(8,128)}, u32[]{:S(2)}) copy-start(f32[3,256,1024]{2,1,0:T(8,128)} %copy-done.16) | copy-start | bytes 9437188
  141.3 3.6 %copy-start.19 = (bf16[1,1024,384]{1,2,0:T(8,128)(2,1)S(1)}, bf16[1,1024,384]{1,2,0:T(8,128)(2,1)}, u32[]{:S(2)}) copy-start(bf16[1,1024,384]{1,2,0:T(8,128)(2,1)} %copy.32) | copy-start | bytes 2359300
  141.3 3.6 %copy-start.27 = (f32[3,256]{1,0:T(4,128)S(1)}, f32[3,256]{1,0:T(4,128)}, u32[]{:S(2)}) copy-start(f32[3,256]{1,0:T(4,128)} %copy-done.26) | copy-start | bytes 9220
  141.3 3.6 %copy-start.29 = (bf16[384,256]{1,0:T(8,128)(2,1)S(1)}, bf16[384,256]{1,0:T(8,128)(2,1)}, u32[]{:S(2)}) copy-start(bf16[384,256]{1,0:T(8,128)(2,1)} %fusion.37) | copy-start | bytes 589828
  153.6 3.1 %copy-start.7 = (bf16[1,1024,384]{1,2,0:T(8,128)(2,1)S(1)}, bf16[1,1024,384]{1,2,0:T(8,128)(2,1)}, u32[]{:S(2)}) copy-start(bf16[1,1024,384]{1,2,0:T(8,128)(2,1)} %copy.28) | copy-start | bytes 2359300
  153.6 3.1 %copy-start.11 = (bf16[3,256,1024]{2,1,0:T(8,128)(2,1)S(1)}, bf16[3,256,1024]{2,1,0:T(8,128)(2,1)}, u32[]{:S(2)}) copy-start(bf16[3,256,1024]{2,1,0:T(8,128)(2,1)} %copy-done.10) | copy-start | bytes 4718596
  160.0 30.0 %copy-start.9 = (f32[256,384]{0,1:T(8,128)S(1)}, f32[256,384]{0,1:T(8,128)}, u32[]{:S(2)}) copy-start(f32[256,384]{0,1:T(8,128)} %copy-done.8) | copy-start | bytes 1179652
  163.2 27.4 %copy-start.14 = (f32[256,384]{1,0:T(8,128)S(1)}, f32[256,384]{1,0:T(8,128)}, u32[]{:S(2)}) copy-start(f32[256,384]{1,0:T(8,128)} %copy.27) | copy-start | bytes 1179652
  163.2 27.4 %copy-start.15 = (f32[256,384]{1,0:T(8,128)S(1)}, f32[256,384]{1,0:T(8,128)}, u32[]{:S(2)}) copy-start(f32[256,384]{1,0:T(8,128)} %copy.26) | copy-start | bytes 1179652
  190.5 1.3 copy-start.20
  190.6 1.3 copy-start.21
  191.8 5.3 %copy-start.23 = (f32[256]{0:T(256)S(1)}, f32[256]{0:T(256)}, u32[]{:S(2)}) copy-start(f32[256]{0:T(256)} %copy-done.22) | copy-start | bytes 3076
  191.8 5.3 %copy-start.25 = (f32[256]{0:T(256)S(1)}, f32[256]{0:T(256)}, u32[]{:S(2)}) copy-start(f32[256]{0:T(256)} %copy-done.24) | copy-start | bytes 3076
  197.2 2.4 copy-start.12
  197.2 4.8 %copy-start.4 = (bf16[3072,384]{0,1:T(8,128)(2,1)S(1)}, bf16[3072,384]{0,1:T(8,128)(2,1)}, u32[]{:S(2)}) copy-start(bf16[3072,384]{0,1:T(8,128)(2,1)} %fusion.4) | copy-start | bytes 7077892
  200.6 24.2 %collective-permute-start = (bf16[256,1536]{1,0:T(8,128)(2,1)}, bf16[256,1536]{1,0:T(8,128)(2,1)}, u32[]{:S(2)}, u32[]{:S(2)}) collective-permute-start(bf16[256,1536]{1,0:T(8,128)(2,1)} %constant_dynamic-slice_fusion), channel_id=1, source_target_pairs={{0,4},{4,0},{1,5},{5,1},{2,6},{6,2},{3,7},{7,3},{8,12},{12,8},{9,1... | collective-permute-start | bytes 2359304 | tf_op jit(solution)/shard_map/ppermute | solution.py:471
  212.0 12.8 %copy-start.5 = (f32[256,3072]{1,0:T(8,128)S(1)}, f32[256,3072]{1,0:T(8,128)}, u32[]{:S(2)}) copy-start(f32[256,3072]{1,0:T(8,128)} %fusion.9) | copy-start | bytes 9437188
  226.6 72.6 %collective-permute-start.1 = (f32[2,256]{1,0:T(2,128)S(1)}, f32[2,256]{1,0:T(2,128)S(1)}, u32[]{:S(2)}, u32[]{:S(2)}) collective-permute-start(f32[2,256]{1,0:T(2,128)S(1)} %pad_maximum_fusion.7), channel_id=1, source_target_pairs={{0,4},{4,0},{1,5},{5,1},{2,6},{6,2},{3,7},{7,3},{8,12},{12,8},{9,1... | collective-permute-start | bytes 6152 | tf_op jit(solution)/shard_map/ppermute | solution.py:471
  227.2 3.7 %copy-start.2 = (bf16[3072,1536]{1,0:T(8,128)(2,1)S(1)}, bf16[3072,1536]{1,0:T(8,128)(2,1)}, u32[]{:S(2)}) copy-start(bf16[3072,1536]{1,0:T(8,128)(2,1)} %copy.42) | copy-start | bytes 28311556
  230.9 68.3 %copy-start.13 = (bf16[256,3072]{1,0:T(8,128)(2,1)S(1)}, bf16[256,3072]{1,0:T(8,128)(2,1)}, u32[]{:S(2)}) copy-start(bf16[256,3072]{1,0:T(8,128)(2,1)} %copy-done.12) | copy-start | bytes 4718596
  297.4 2.3 copy-start.6
  298.2 3.9 %copy-start.1 = (bf16[1,256,3072]{2,1,0:T(8,128)(2,1)S(1)}, bf16[1,256,3072]{2,1,0:T(8,128)(2,1)}, u32[]{:S(2)}) copy-start(bf16[1,256,3072]{2,1,0:T(8,128)(2,1)} %param.5) | copy-start | bytes 4718596
  (2 other events, 2.3 us)
Sparse Core Ops, SparseCore 0:
  92.3 35.5 all-gather.1
  153.7 34.2 reduce-scatter.1
where the time goes:
time: 314 us; the launch traced here: 309 us
  Pallas kernels  130 us (41%)
  waiting for transfers between devices  55.9 us (18%)
  local copies, waits for them, and re-layouts  45.9 us (15%)
  other arithmetic  30.6 us (10%)
  matrix products  29.9 us (10%)
  between operations  14.5 us (5%)
    pallas_call x1, Pallas kernels, scatter_rows(): pl.pallas_call(functools.partial(scatter_kernel, seq_count, dp_count), ou...  66.5 us
    pallas_call x1, Pallas kernels, gather_rows(): pl.pallas_call(functools.partial(gather_kernel, seq_count, dp_count), out...  63.3 us
    all_gather x1, waiting for transfers between devices, local(): every_pair = lax.all_gather(key_value, 'seq', axis=1, tiled=True)  31 us
    reduce_scatter x1, waiting for transfers between devices, local(): lax.psum_scatter(every_grad.astype(jnp.bfloat16), 'seq', scatter_dimensio...  24.9 us
    concatenate x1, local copies, waits for them, and re-layouts, local(): terms = jnp.concatenate([qkv_term, out_term], axis=1)  12.8 us
    concatenate x1, other arithmetic, local(): terms = jnp.concatenate([qkv_term, out_term], axis=1)  9.91 us
  transfers between devices with their start and end apart: 4, of which 2 were waited for; matrix products, arithmetic and copies ran while one was open for 12% of the time, Pallas kernels for 22%

commit v1 on v0

v1 whole, which is shorter than its diff:
```python
import functools

import jax
import jax.numpy as jnp
from jax import lax
from jax.experimental import pallas as pl
from jax.experimental.pallas import tpu as pltpu
from jax.sharding import PartitionSpec as P

HD = 128
CORES = 2
MESH_ID = pl.DeviceIdType.MESH
EPSILON = 1e-06
F32, BF16 = jnp.float32, jnp.bfloat16


def dot(left, right):
    return jnp.dot(left, right, preferred_element_type=F32)


def dot_nt(left, right):
    return lax.dot_general(left, right, (((1,), (1,)), ((), ())), preferred_element_type=F32)


def dot_tn(left, right):
    return lax.dot_general(left, right, (((0,), (0,)), ((), ())), preferred_element_type=F32)


def normalize(values):
    centered = values - jnp.mean(values, axis=-1, keepdims=True)
    inverse = lax.rsqrt(jnp.mean(centered * centered, axis=-1, keepdims=True) + EPSILON)
    return centered * inverse, inverse


def normalize_back(gradient, normed, inverse):
    mean_grad = jnp.mean(gradient, axis=-1, keepdims=True)
    mean_both = jnp.mean(gradient * normed, axis=-1, keepdims=True)
    return (gradient - mean_grad - normed * mean_both) * inverse


def body(
    sizes,
    tokens_hbm,
    cotangent_hbm,
    qkv_hbm,
    outw_hbm,
    qkv_out,
    outw_out,
    branch_out,
    tok,
    cot,
    unit_low,
    unit_t,
    cot_t,
    stat_mean,
    stat_inv,
    w_kv,
    w_qo,
    acc_kv,
    acc_qo,
    pairs,
    query_low,
    query_unit,
    key_unit,
    query_inv,
    key_inv,
    grad_low,
    expo,
    totals,
    deltas,
    weighted,
    attended,
    query_raw,
    part,
    part_in,
    back_q,
    back_kv,
    inner,
    inner_in,
    sums,
    sums_in,
    term_kv,
    term_qo,
    core_kv,
    core_qo,
    chip_kv,
    chip_qo,
    chain_kv,
    chain_qo,
    load_sem,
    w_recv,
    w_right,
    w_left,
    w_chip,
    w_core,
    p_recv,
    p_right,
    p_left,
    g_low,
    g_high,
    g_send,
    t_core_send,
    t_core_recv,
    t_chip_send,
    t_chip_recv,
    t_chain_send,
    t_low_recv,
    t_high_recv,
    x_send,
    x_recv,
    xs_send,
    xs_recv,
):
    seq_count, dp_count, tensor_count, own_rows, head_count = sizes
    chip_count = dp_count // CORES
    token_count, feature_count = tok.shape
    columns = head_count * HD
    share = feature_count // tensor_count
    plane = dp_count * own_rows
    scale = HD ** (-0.5)
    place = lax.axis_index("seq")
    index = lax.axis_index("dp")
    lane = lax.axis_index("tensor")
    chip, core = index // CORES, index % CORES
    not_last, not_first = place < seq_count - 1, place > 0
    weights, terms = (w_kv, w_qo), (term_kv, term_qo)
    held, chip_in = (core_kv, core_qo), (chip_kv, chip_qo)
    chain_in = (chain_kv, chain_qo)
    KV, QO = 0, 1

    own_slot = place * dp_count + index

    def rows_of(slot):
        return pl.ds(pl.multiple_of(slot * own_rows, own_rows), own_rows)

    loads = [
        pltpu.make_async_copy(
            qkv_hbm.at[pl.ds(1, 2)], w_kv.at[:, rows_of(own_slot), :], load_sem.at[0]
        ),
        pltpu.make_async_copy(qkv_hbm.at[0], w_qo.at[0, rows_of(own_slot), :], load_sem.at[1]),
        pltpu.make_async_copy(outw_hbm, w_qo.at[1, rows_of(own_slot), :], load_sem.at[2]),
        pltpu.make_async_copy(tokens_hbm, tok, load_sem.at[3]),
        pltpu.make_async_copy(cotangent_hbm, cot, load_sem.at[4]),
    ]
    for load in loads:
        load.start()

    barrier = pltpu.get_barrier_semaphore()

    def signal(device):
        pl.semaphore_signal(barrier, inc=1, device_id=device, device_id_type=MESH_ID)

    @pl.when(not_first)
    def _():
        signal({"seq": place - 1})

    @pl.when(not_last)
    def _():
        signal({"seq": place + 1})

    for step in range(1, chip_count):
        signal({"dp": (chip + step) % chip_count * CORES + core})
    signal({"dp": chip * CORES + 1 - core})
    for step in range(1, tensor_count):
        signal({"tensor": (lane + step) % tensor_count})
    ends = jnp.minimum(place, 1) + jnp.minimum(seq_count - 1 - place, 1)
    pl.semaphore_wait(barrier, chip_count + tensor_count - 1 + ends)

    def remote(source, target, send_sem, recv_sem, device):
        return pltpu.make_async_remote_copy(
            src_ref=source,
            dst_ref=target,
            send_sem=send_sem,
            recv_sem=recv_sem,
            device_id=device,
            device_id_type=MESH_ID,
        )

    up, down = {"seq": place + 1}, {"seq": place - 1}
    beside_device = {"dp": chip * CORES + 1 - core}

    def chip_device(step):
        return {"dp": (chip + step) % chip_count * CORES + core}

    both_sides = jnp.minimum(place, seq_count - 1 - place)

    def origin_at(k):
        if k == 0:
            return place
        near = place - (k + 1) // 2 if k % 2 else place + k // 2
        far = jnp.where(place * 2 > seq_count - 1, place - (k - both_sides), place + (k - both_sides))
        return jnp.where(k <= 2 * both_sides, near, far)

    def w_copy(half, slot, send_sem, device):
        ref = weights[half].at[:, rows_of(slot), :]
        return remote(ref, ref, send_sem, w_recv.at[half, slot], device)

    def w_side(half, origin, rightward):
        if rightward:
            return w_copy(half, origin * dp_count + index, w_right.at[half, origin], up)
        return w_copy(half, origin * dp_count + index, w_left.at[half, origin], down)

    def w_across(half, origin, step):
        sem = w_chip.at[half, origin * chip_count + step]
        return w_copy(half, origin * dp_count + index, sem, chip_device(step))

    def w_beside(half, origin, source_chip):
        sem = w_core.at[half, origin * chip_count + source_chip]
        return w_copy(half, origin * dp_count + source_chip * CORES + core, sem, beside_device)

    def w_landed(half, slot):
        w_copy(half, slot, w_core.at[half, 0], beside_device).wait_recv()

    def w_sides_own(half):
        @pl.when(not_last)
        def _():
            w_side(half, place, True).start()

        @pl.when(not_first)
        def _():
            w_side(half, place, False).start()

    def w_spread(half, origin):
        for step in range(1, chip_count):
            w_across(half, origin, step).start()

    def w_step(half, k):
        origin = origin_at(k)
        w_landed(half, origin * dp_count + index)

        @pl.when((origin < place) & not_last)
        def _():
            w_side(half, origin, True).start()

        @pl.when((origin > place) & not_first)
        def _():
            w_side(half, origin, False).start()

        w_spread(half, origin)
        w_beside(half, origin, chip).start()

    def w_chip_step(half, k):
        origin = origin_at(k)
        for step in range(1, chip_count):
            source_chip = (chip + step) % chip_count
            w_landed(half, origin * dp_count + source_chip * CORES + core)
            w_beside(half, origin, source_chip).start()

    def project(half, k):
        origin = origin_at(k)
        for source_chip in range(chip_count):
            w_landed(half, origin * dp_count + source_chip * CORES + 1 - core)
        rows = pl.ds(pl.multiple_of(origin * plane, plane), plane)
        acc = (acc_kv, acc_qo)[half]
        for j in range(2):
            source = cot if (half == QO and j == 1) else unit_low
            product = dot(source[:, rows], weights[half][j, rows, :])
            if k == 0:
                acc[j] = product
            else:
                acc[j] += product

    def block_rows(origin):
        return pl.ds(pl.multiple_of(origin * token_count, token_count), token_count)

    def p_copy(origin, rightward):
        ref = pairs.at[:, block_rows(origin), :]
        if rightward:
            return remote(ref, ref, p_right.at[origin], p_recv.at[origin], up)
        return remote(ref, ref, p_left.at[origin], p_recv.at[origin], down)

    def p_step(k):
        origin = origin_at(k)
        p_copy(origin, True).wait_recv()

        @pl.when((origin < place) & not_last)
        def _():
            p_copy(origin, True).start()

        @pl.when((origin > place) & not_first)
        def _():
            p_copy(origin, False).start()

    loads[0].wait()
    w_sides_own(KV)
    w_spread(KV, place)
    w_beside(KV, place, chip).start()
    loads[1].wait()
    loads[2].wait()
    loads[3].wait()
    loads[4].wait()

    @pl.loop(0, token_count // 32)
    def _(step):
        rows = pl.ds(pl.multiple_of(step * 32, 32), 32)
        values = tok[rows, :].astype(F32)
        average = jnp.mean(values, axis=-1, keepdims=True)
        centered = values - average
        inverse = lax.rsqrt(jnp.mean(centered * centered, axis=-1, keepdims=True) + EPSILON)
        unit_low[rows, :] = (centered * inverse).astype(BF16)
        stat_mean[rows, :] = jnp.broadcast_to(average, (32, 128))
        stat_inv[rows, :] = jnp.broadcast_to(inverse, (32, 128))

    def flip(source, target):
        @pl.loop(0, feature_count // 128)
        def _(step):
            cut = pl.ds(pl.multiple_of(step * 128, 128), 128)
            target[cut, :] = source[:, cut].T

    fill = [lambda: flip(unit_low, unit_t), lambda: flip(cot, cot_t)]
    own_qo_at = min(2, seq_count - 1)
    for k in range(1, seq_count):
        w_step(KV, k)
        if k == own_qo_at:
            w_sides_own(QO)
            w_beside(QO, place, chip).start()
        if k == seq_count - 1:
            w_spread(QO, place)
        w_chip_step(KV, k - 1)
        project(KV, k - 1)
        if fill:
            fill.pop(0)()
    for rest in fill:
        rest()
    w_chip_step(KV, seq_count - 1)
    project(KV, seq_count - 1)

    own_block = block_rows(place)
    for h in range(head_count):
        cut = slice(h * HD, (h + 1) * HD)
        normed, inverse = normalize(acc_kv[0, :, cut])
        key_unit[:, cut] = normed
        key_inv[:, cut] = jnp.broadcast_to(inverse, (token_count, HD))
        pairs[0, own_block, cut] = normed.astype(BF16)
        pairs[1, own_block, cut] = acc_kv[1, :, cut].astype(BF16)

    for k in range(1, min(3, seq_count)):
        w_step(QO, k)

    @pl.when(not_last)
    def _():
        p_copy(place, True).start()

    @pl.when(not_first)
    def _():
        p_copy(place, False).start()

    w_chip_step(QO, 0)
    project(QO, 0)
    for k in range(3, seq_count):
        w_step(QO, k)
    for k in range(1, seq_count - 1):
        w_chip_step(QO, k)
        project(QO, k)
    if seq_count > 1:
        p_step(1)
    if seq_count > 1:
        w_chip_step(QO, seq_count - 1)
        project(QO, seq_count - 1)
    for h in range(head_count):
        cut = slice(h * HD, (h + 1) * HD)
        normed, inverse = normalize(acc_qo[0, :, cut])
        query_unit[:, cut] = normed
        query_inv[:, cut] = jnp.broadcast_to(inverse, (token_count, HD))
        query_low[:, cut] = normed.astype(BF16)
    grad_low[...] = acc_qo[1].astype(BF16)

    def head_cut(h):
        return pl.ds(pl.multiple_of(h * HD, HD), HD)

    def expo_at(origin, h):
        row = (h * seq_count + origin) * token_count
        return pl.ds(pl.multiple_of(row, token_count), token_count)

    def attend(k):
        origin = origin_at(k)

        @pl.loop(0, head_count)
        def _(h):
            cut = head_cut(h)
            rows = block_rows(origin)
            scores = dot_nt(query_low[:, cut], pairs[0, rows, cut]) * scale
            exponent = jnp.exp(scores)
            low = exponent.astype(BF16)
            expo[expo_at(origin, h), :] = low
            total = exponent[:, :HD]
            for at in range(HD, token_count, HD):
                total = total + exponent[:, at : at + HD]
            mixed = dot(low, pairs[1, rows, cut])
            if k == 0:
                totals[h] = total
                weighted[:, cut] = mixed
            else:
                totals[h] += total
                weighted[:, cut] += mixed

    attend(0)
    for k in range(1, seq_count):
        if k > 1:
            p_step(k)
        attend(k)
    for h in range(head_count):
        cut = slice(h * HD, (h + 1) * HD)
        total = jnp.sum(totals[h], axis=-1, keepdims=True)
        low = (weighted[:, cut] / total).astype(BF16)
        attended[:, cut] = low
        both = grad_low[:, cut].astype(F32) * low.astype(F32)
        totals[h] = jnp.broadcast_to(1.0 / total, (token_count, HD))
        deltas[h] = jnp.broadcast_to(jnp.sum(both, axis=-1, keepdims=True), (token_count, HD))

    order = []
    for turn in range((seq_count + 1) // 2):
        order.extend(sorted({seq_count - 1 - turn, turn}, reverse=True))
    mirror = jnp.where(place * 2 < seq_count, 0, 1)

    def target_at(n):
        return order[n] + mirror * (seq_count - 1 - 2 * order[n])

    def from_above(target, receiver):
        return jnp.where(target == receiver, seq_count, target)

    def g_copy(target, rightward):
        rows = block_rows(target)
        source = part.at[:, rows, :]
        if rightward:
            into, sem, device = rows, g_low, up
        else:
            into, sem, device = block_rows(from_above(target, place - 1)), g_high, down
        return remote(source, part_in.at[:, into, :], g_send.at[target], sem.at[target], device)

    def backward(n):
        target = target_at(n)

        @pl.loop(0, head_count)
        def _(h):
            cut = head_cut(h)
            rows = block_rows(target)
            inv_total = totals[h][:, :1]
            probability = expo[expo_at(target, h), :].astype(F32) * inv_total
            gradient = grad_low[:, cut]
            prob_grad = dot_nt(gradient, pairs[1, rows, cut])
            score = (probability * (prob_grad - deltas[h][:, :1]) * scale).astype(BF16)
            query_part = dot(score, pairs[0, rows, cut])
            part[0, rows, cut] = dot_tn(score, query_low[:, cut]).astype(BF16)
            part[1, rows, cut] = dot_tn(probability.astype(BF16), gradient).astype(BF16)
            if n == 0:
                query_raw[:, cut] = query_part
            else:
                query_raw[:, cut] += query_part

    for n in range(seq_count):
        backward(n)
        target = target_at(n)

        @pl.when((target > place) & (place == 0))
        def _():
            g_copy(target, True).start()

        @pl.when((target < place) & (place == seq_count - 1))
        def _():
            g_copy(target, False).start()

    for h in range(head_count):
        cut = slice(h * HD, (h + 1) * HD)
        raised = normalize_back(query_raw[:, cut], query_unit[:, cut], query_inv[:, cut])
        back_q[:, cut] = raised.astype(BF16)

    def t_piece(ref, slot):
        return ref.at[:, rows_of(slot), :]

    def t_beside(half, target, target_chip):
        slot = target * chip_count + target_chip
        source = t_piece(terms[half], target * dp_count + target_chip * CORES + 1 - core)
        into = t_piece(held[half], slot)
        sems = t_core_send.at[half, slot], t_core_recv.at[half, slot]
        return remote(source, into, *sems, beside_device)

    def t_across(half, target, step):
        other = (chip + step) % chip_count
        slot = (step - 1) * seq_count + target
        source = t_piece(held[half], target * chip_count + other)
        into = t_piece(chip_in[half], slot)
        sems = t_chip_send.at[half, slot], t_chip_recv.at[half, slot]
        return remote(source, into, *sems, chip_device(step))

    def t_chain(half, target, rightward):
        source = t_piece(held[half], target * chip_count + chip)
        if rightward:
            at, sem, device = target, t_low_recv, up
        else:
            at, sem, device = from_above(target, place - 1), t_high_recv, down
        send_sem = t_chain_send.at[half, target]
        into = t_piece(chain_in[half], at)
        return remote(source, into, send_sem, sem.at[half, target], device)

    def add_into(ref, slot, others, size):
        @pl.loop(0, size // 16)
        def _(step):
            def cut(at):
                return pl.ds(pl.multiple_of(at * size + step * 16, 16), 16)

            for j in range(2):
                total = ref[j, cut(slot), :].astype(F32)
                for other, at in others:
                    total = total + other[j, cut(at), :].astype(F32)
                ref[j, cut(slot), :] = total.astype(BF16)

    def make_terms(half, n):
        target = target_at(n)

        @pl.loop(0, dp_count)
        def _(at):
            rows = rows_of(target * dp_count + at)
            for j in range(2):
                if half == KV:
                    product = dot(unit_t[rows, :], back_kv[j])
                elif j == 0:
                    product = dot(unit_t[rows, :], back_q[...])
                else:
                    product = dot(cot_t[rows, :], attended[...])
                terms[half][j, rows, :] = product.astype(BF16)

        for step in range(1, chip_count):
            t_beside(half, target, (chip + step) % chip_count).start()
        t_beside(half, target, chip).start()

    def send_across(half, n):
        target = target_at(n)
        for step in range(1, chip_count):
            other = (chip + step) % chip_count
            t_beside(half, target, other).wait_recv()
            slot = target * chip_count + other
            add_into(
                held[half], slot, [(terms[half], target * dp_count + other * CORES + core)], own_rows
            )
            t_across(half, target, step).start()

    def chain(half, n):
        target = target_at(n)
        slot = target * chip_count + chip
        t_beside(half, target, chip).wait_recv()
        others = [(terms[half], target * dp_count + index)]
        for step in range(1, chip_count):
            t_across(half, target, step).wait_recv()
            others.append((chip_in[half], (step - 1) * seq_count + target))
        add_into(held[half], slot, others, own_rows)

        @pl.when(place < target)
        def _():
            @pl.when(not_first)
            def _():
                t_chain(half, target, True).wait_recv()
                add_into(held[half], slot, [(chain_in[half], target)], own_rows)

            t_chain(half, target, True).start()

        @pl.when(place > target)
        def _():
            @pl.when(not_last)
            def _():
                t_chain(half, target, False).wait_recv()
                add_into(held[half], slot, [(chain_in[half], target)], own_rows)

            t_chain(half, target, False).start()

    for n in range(seq_count):
        make_terms(QO, n)
    for n in range(seq_count):
        send_across(QO, n)

    for n in range(seq_count):
        target = target_at(n)

        @pl.when((place < target) & not_first)
        def _():
            g_copy(target, True).wait_recv()
            add_into(part, target, [(part_in, target)], token_count)
            g_copy(target, True).start()

        @pl.when((place > target) & not_last)
        def _():
            g_copy(target, False).wait_recv()
            add_into(part, target, [(part_in, target)], token_count)
            g_copy(target, False).start()

    @pl.when(not_first)
    def _():
        g_copy(place, True).wait_recv()
        add_into(part, place, [(part_in, place)], token_count)

    @pl.when(not_last)
    def _():
        g_copy(place, False).wait_recv()
        add_into(part, place, [(part_in, seq_count)], token_count)

    for h in range(head_count):
        cut = slice(h * HD, (h + 1) * HD)
        raw = part[0, own_block, cut].astype(F32)
        raised = normalize_back(raw, key_unit[:, cut], key_inv[:, cut])
        back_kv[0, :, cut] = raised.astype(BF16)
        back_kv[1, :, cut] = part[1, own_block, cut]

    for n in range(seq_count):
        make_terms(KV, n)
    for n in range(seq_count):
        send_across(KV, n)

    width = next(size for size in (512, 384, 256, 128) if share % size == 0)
    sums[...] = jnp.zeros_like(sums)

    def lanes(values):
        total = values[:, :128]
        for at in range(128, width, 128):
            total = total + values[:, at : at + 128]
        return total

    @pl.loop(0, feature_count // width)
    def _(step):
        cut = pl.ds(pl.multiple_of(step * width, width), width)
        product = dot_nt(back_q[...], w_qo[0, cut, :])
        product = product + dot_nt(back_kv[0], w_kv[0, cut, :])
        product = product + dot_nt(back_kv[1], w_kv[1, cut, :])
        unit = (tok[:, cut].astype(F32) - stat_mean[:, :1]) * stat_inv[:, :1]
        sums[0] += lanes(product)
        sums[1] += lanes(product * unit)
        inner[step // (share // width), :, pl.ds(
            pl.multiple_of(step % (share // width) * width, width), width
        )] = product.astype(BF16)

    def x_copy(step):
        other = (lane + step) % tensor_count
        return remote(
            inner.at[other],
            inner_in.at[step - 1],
            x_send.at[step - 1],
            x_recv.at[step - 1],
            {"tensor": other},
        )

    def xs_copy(step):
        other = (lane + step) % tensor_count
        return remote(
            sums,
            sums_in.at[step - 1],
            xs_send.at[step - 1],
            xs_recv.at[step - 1],
            {"tensor": other},
        )

    for step in range(1, tensor_count):
        x_copy(step).start()
        xs_copy(step).start()
    for n in range(seq_count):
        chain(QO, n)

    def finish_branch():
        for step in range(1, tensor_count):
            x_copy(step).wait_recv()
            xs_copy(step).wait_recv()

        @pl.loop(0, token_count // 16)
        def _(step):
            rows = pl.ds(pl.multiple_of(step * 16, 16), 16)
            first, second = sums[0, rows, :], sums[1, rows, :]
            values = inner[lane, rows, :].astype(F32)
            for other in range(tensor_count - 1):
                first = first + sums_in[other, 0, rows, :]
                second = second + sums_in[other, 1, rows, :]
                values = values + inner_in[other, rows, :].astype(F32)
            mean_grad = jnp.sum(first, axis=-1, keepdims=True) / feature_count
            mean_both = jnp.sum(second, axis=-1, keepdims=True) / feature_count
            cut = pl.ds(pl.multiple_of(lane * share, share), share)
            inverse = stat_inv[rows, :][:, :1]
            unit = (tok[rows, cut].astype(F32) - stat_mean[rows, :][:, :1]) * inverse
            branch_out[rows, :] = ((values - mean_grad - unit * mean_both) * inverse).astype(BF16)

    for n in range(seq_count):
        chain(KV, n)
    finish_branch()

    own_held = place * chip_count + chip
    for half in (QO, KV):

        @pl.when(not_first)
        def _():
            t_chain(half, place, True).wait_recv()

        @pl.when(not_last)
        def _():
            t_chain(half, place, False).wait_recv()

        @pl.loop(0, own_rows // 16)
        def _(step):
            rows = pl.ds(pl.multiple_of(step * 16, 16), 16)

            def cut(at):
                return pl.ds(pl.multiple_of(at * own_rows + step * 16, 16), 16)

            for j in range(2):
                if half == KV:
                    target = qkv_out.at[1 + j]
                else:
                    target = outw_out if j else qkv_out.at[0]
                target[rows, :] = held[half][j, cut(own_held), :].astype(F32)

                @pl.when(not_first)
                def _():
                    target[rows, :] += chain_in[half][j, cut(place), :].astype(F32)

                @pl.when(not_last)
                def _():
                    target[rows, :] += chain_in[half][j, cut(seq_count), :].astype(F32)

    for origin in range(seq_count):
        to_right = (origin <= place) & not_last
        to_left = (origin >= place) & not_first
        for half in (KV, QO):
            for step in range(1, chip_count):
                w_across(half, origin, step).wait_send()
                t_across(half, origin, step).wait_send()
            for source_chip in range(chip_count):
                w_beside(half, origin, source_chip).wait_send()
                t_beside(half, origin, source_chip).wait_send()

            @pl.when(to_right)
            def _():
                w_side(half, origin, True).wait_send()

            @pl.when(to_left)
            def _():
                w_side(half, origin, False).wait_send()

            @pl.when(place != origin)
            def _():
                t_chain(half, origin, True).wait_send()

        @pl.when(to_right)
        def _():
            p_copy(origin, True).wait_send()

        @pl.when(to_left)
        def _():
            p_copy(origin, False).wait_send()

        @pl.when(place != origin)
        def _():
            g_copy(origin, True).wait_send()

    for step in range(1, tensor_count):
        x_copy(step).wait_send()
        xs_copy(step).wait_send()


def local(tokens, cotangent, qkv_weight, out_weight):
    seq_count, dp_count = lax.axis_size("seq"), lax.axis_size("dp")
    tensor_count = lax.axis_size("tensor")
    chip_count = dp_count // CORES
    row_count, feature_count = tokens.shape[1:]
    own_rows, columns = out_weight.shape
    head_count = columns // HD
    share = feature_count // tensor_count
    sizes = (seq_count, dp_count, tensor_count, own_rows, head_count)

    def vmem(*shape, kind=BF16):
        return pltpu.VMEM(shape, kind)

    def dma(*shape):
        return pltpu.SemaphoreType.DMA(shape)

    both, peers = seq_count * chip_count, seq_count * (chip_count - 1)
    scratch = [
        vmem(row_count, feature_count),
        vmem(row_count, feature_count),
        vmem(row_count, feature_count),
        vmem(feature_count, row_count),
        vmem(feature_count, row_count),
        vmem(row_count, 128, kind=F32),
        vmem(row_count, 128, kind=F32),
        vmem(2, feature_count, columns),
        vmem(2, feature_count, columns),
        vmem(2, row_count, columns, kind=F32),
        vmem(2, row_count, columns, kind=F32),
        vmem(2, seq_count * row_count, columns),
        vmem(row_count, columns),
        vmem(row_count, columns, kind=F32),
        vmem(row_count, columns, kind=F32),
        vmem(row_count, columns, kind=F32),
        vmem(row_count, columns, kind=F32),
        vmem(row_count, columns),
        vmem(head_count * seq_count * row_count, row_count),
        vmem(head_count, row_count, HD, kind=F32),
        vmem(head_count, row_count, HD, kind=F32),
        vmem(row_count, columns, kind=F32),
        vmem(row_count, columns),
        vmem(row_count, columns, kind=F32),
        vmem(2, seq_count * row_count, columns),
        vmem(2, (seq_count + 1) * row_count, columns),
        vmem(row_count, columns),
        vmem(2, row_count, columns),
        vmem(tensor_count, row_count, share),
        vmem(max(tensor_count - 1, 1), row_count, share),
        vmem(2, row_count, 128, kind=F32),
        vmem(max(tensor_count - 1, 1), 2, row_count, 128, kind=F32),
        vmem(2, feature_count, columns),
        vmem(2, feature_count, columns),
        vmem(2, both * own_rows, columns),
        vmem(2, both * own_rows, columns),
        vmem(2, max(peers, 1) * own_rows, columns),
        vmem(2, max(peers, 1) * own_rows, columns),
        vmem(2, (seq_count + 1) * own_rows, columns),
        vmem(2, (seq_count + 1) * own_rows, columns),
        dma(5),
        dma(2, seq_count * dp_count),
        dma(2, seq_count),
        dma(2, seq_count),
        dma(2, both),
        dma(2, both),
        dma(seq_count),
        dma(seq_count),
        dma(seq_count),
        dma(seq_count),
        dma(seq_count),
        dma(seq_count),
        dma(2, both),
        dma(2, both),
        dma(2, max(peers, 1)),
        dma(2, max(peers, 1)),
        dma(2, seq_count),
        dma(2, seq_count),
        dma(2, seq_count),
        dma(max(tensor_count - 1, 1)),
        dma(max(tensor_count - 1, 1)),
        dma(max(tensor_count - 1, 1)),
        dma(max(tensor_count - 1, 1)),
    ]
    anywhere = pl.BlockSpec(memory_space=pl.ANY)
    vector = pl.BlockSpec(memory_space=pltpu.VMEM)
    qkv_grad, out_grad, branch = pl.pallas_call(
        functools.partial(body, sizes),
        out_shape=(
            jax.ShapeDtypeStruct((3, own_rows, columns), F32),
            jax.ShapeDtypeStruct((own_rows, columns), F32),
            jax.ShapeDtypeStruct((row_count, share), BF16),
        ),
        in_specs=[anywhere] * 4,
        out_specs=(vector, vector, vector),
        scratch_shapes=scratch,
        compiler_params=pltpu.CompilerParams(
            collective_id=0, has_side_effects=True, vmem_limit_bytes=67043328
        ),
        name="layer",
    )(tokens[0], cotangent[0], jnp.transpose(qkv_weight, (1, 0, 2)), out_weight)
    return jnp.transpose(qkv_grad, (1, 0, 2)), out_grad, branch[None]


def solution(mesh):
    return jax.shard_map(
        local,
        mesh=mesh,
        in_specs=(
            P("dp", "seq", None),
            P("dp", "seq", None),
            P(("seq", "dp"), None, "tensor"),
            P(("seq", "dp"), "tensor"),
        ),
        out_specs=(
            P(("seq", "dp"), None, "tensor"),
            P(("seq", "dp"), "tensor"),
            P("dp", "seq", "tensor"),
        ),
        check_vma=False,
    )
```

time: 314 us -> 174 us (0.55); the launches traced: 309 us -> 174 us
  waiting for transfers between devices: 55.9 us -> 0 us
  local copies, waits for them, and re-layouts: 45.9 us -> 3.83 us
  Pallas kernels: 130 us -> 169 us
  other arithmetic: 30.6 us -> 0 us
  matrix products: 29.9 us -> 0 us
  between operations: 14.5 us -> 0.66 us
    pallas_call x2 -> x1, Pallas kernels: 130 us -> 169 us  [local(): pl.pallas_call(functools.partial(body, sizes), out_shape=(jax.ShapeDtypeS...]
    all_gather x1 -> x0, waiting for transfers between devices: 31 us -> none  [local(): every_pair = lax.all_gather(key_value, 'seq', axis=1, tiled=True)]
    dot_general x11 -> x0, matrix products: 29.9 us -> none  [the longest x1 5.31 us: local(): jnp.einsum('rc,dc->rd', qkv_low, full_qkv, preferred_element_type=jnp.flo...]
    reduce_scatter x1 -> x0, waiting for transfers between devices: 24.9 us -> none  [local(): lax.psum_scatter(every_grad.astype(jnp.bfloat16), 'seq', scatter_dimensio...]
    concatenate x1 -> x0, local copies, waits for them, and re-layouts: 12.8 us -> none  [local(): terms = jnp.concatenate([qkv_term, out_term], axis=1)]
    concatenate x2 -> x0, other arithmetic: 11.7 us -> none  [the longest x1 9.91 us: local(): terms = jnp.concatenate([qkv_term, out_term], axis=1)]
    slice x10 -> x0, local copies, waits for them, and re-layouts: 11.3 us -> none  [the longest x2 4.95 us: local(): value_rows = every_pair[1].reshape(piece_rows, head_count, HD)]
    another operation x5 -> x0, other arithmetic: 6.53 us -> none  [the longest x1 2.79 us: local(): jnp.stack([key_part.reshape(piece_rows, column_count), value_part.reshape...]
  transfers between devices with their start and end apart: 4 -> 0, of which waited for: 2 -> 0; matrix products, arithmetic and copies ran while one was open for 12% -> 0% of each run, Pallas kernels for 22% -> 0%
where the time goes in v1:
time: 174 us
  Pallas kernels  169 us (97%)
  local copies, waits for them, and re-layouts  3.83 us (2%)
    pallas_call x1, Pallas kernels, local(): pl.pallas_call(functools.partial(body, sizes), out_shape=(jax.ShapeDtypeS...  169 us
    unnamed x7, local copies, waits for them, and re-layouts  3.83 us

profile of v1, /device:TPU:0, one launch (start us, length us, event | category | flops | bytes accessed | tf_op | source)
XLA Modules:
  0.0 173.8 jit_solution(4420393092718386754)
XLA Ops:
  0.6 169.4 %layer.1 = (f32[3,192,384]{2,1,0:T(8,128)}, f32[192,384]{1,0:T(8,128)}, bf16[256,1536]{1,0:T(8,128)(2,1)}) custom-call(bf16[256,3072]{1,0:T(8,128)(2,1)} %bitcast.5, bf16[256,3072]{1,0:T(8,128)(2,1)} %bitcast.6, bf16[3,192,384]{2,1,0:T(8,128)(2,1)} %bitcast.9, bf16[192,384]{1,0:T(8,128)(2,1)} %outw_hbm.1), custom_call_target="tpu_custom_call" | custom-call | tf_op jit(solution)/shard_map/layer/pallas_call | solution.py:838
  170.0 0.0 copy-start.1
  170.0 0.0 copy-start
  170.0 2.2 %copy.10 = f32[192,3,384]{2,0,1:T(8,128)} copy(f32[192,3,384]{2,0,1:T(8,128)} %bitcast.7) | data formatting | bytes 1769472
  172.2 0.0 copy-done.1
  172.2 0.7 copy.11
  173.0 0.0 copy-done
  173.0 0.9 copy.12
Async XLA Ops:
  170.0 2.2 %copy-start.1 = (f32[192,384]{1,0:T(8,128)S(1)}, f32[192,384]{1,0:T(8,128)}, u32[]{:S(2)}) copy-start(f32[192,384]{1,0:T(8,128)} %get-tuple-element.13) | copy-start | bytes 884740
  170.0 3.0 %copy-start = (bf16[256,1536]{1,0:T(8,128)(2,1)S(1)}, bf16[256,1536]{1,0:T(8,128)(2,1)}, u32[]{:S(2)}) copy-start(bf16[256,1536]{1,0:T(8,128)(2,1)} %get-tuple-element.8) | copy-start | bytes 2359300

commit v2 on v1

v2 whole, which is shorter than its diff:
```python
import functools

import jax
import jax.numpy as jnp
from jax import lax
from jax.experimental import pallas as pl
from jax.experimental.pallas import tpu as pltpu
from jax.sharding import PartitionSpec as P

HD = 128
CORES = 2
MESH_ID = pl.DeviceIdType.MESH
EPSILON = 1e-06
F32, BF16 = jnp.float32, jnp.bfloat16


def dot(left, right):
    return jnp.dot(left, right, preferred_element_type=F32)


def dot_nt(left, right):
    return lax.dot_general(left, right, (((1,), (1,)), ((), ())), preferred_element_type=F32)


def dot_tn(left, right):
    return lax.dot_general(left, right, (((0,), (0,)), ((), ())), preferred_element_type=F32)


def normalize(values):
    centered = values - jnp.mean(values, axis=-1, keepdims=True)
    inverse = lax.rsqrt(jnp.mean(centered * centered, axis=-1, keepdims=True) + EPSILON)
    return centered * inverse, inverse


def normalize_back(gradient, normed, inverse):
    mean_grad = jnp.mean(gradient, axis=-1, keepdims=True)
    mean_both = jnp.mean(gradient * normed, axis=-1, keepdims=True)
    return (gradient - mean_grad - normed * mean_both) * inverse


def body(
    sizes,
    tokens_hbm,
    cotangent_hbm,
    qkv_hbm,
    outw_hbm,
    qkv_out,
    outw_out,
    branch_hbm,
    tok,
    cot,
    unit_low,
    unit_t,
    cot_t,
    stat_mean,
    stat_inv,
    weights,
    acc,
    pairs,
    query_low,
    query_unit,
    key_unit,
    query_inv,
    key_inv,
    grad_low,
    expo,
    totals,
    deltas,
    weighted,
    attended,
    query_raw,
    part,
    part_in,
    back,
    inner,
    inner_in,
    sums,
    terms,
    held,
    chip_in,
    chain_in,
    summed,
    branch_out,
    sum_rows,
    sum_rows_in,
    sum_columns,
    load_sem,
    store_sem,
    w_recv,
    w_right,
    w_left,
    w_chip,
    w_core,
    p_recv,
    p_right,
    p_left,
    g_low,
    g_high,
    g_send,
    t_core_send,
    t_core_recv,
    t_chip_send,
    t_chip_recv,
    t_chain_send,
    t_low_recv,
    t_high_recv,
    x_send,
    x_recv,
    xs_send,
    xs_recv,
):
    seq_count, dp_count, tensor_count, own_rows, head_count = sizes
    chip_count = dp_count // CORES
    token_count, feature_count = tok.shape
    share = feature_count // tensor_count
    plane = dp_count * own_rows
    scale = HD ** (-0.5)
    place = lax.axis_index("seq")
    index = lax.axis_index("dp")
    lane = lax.axis_index("tensor")
    chip, core = index // CORES, index % CORES
    not_last, not_first = place < seq_count - 1, place > 0
    both_sides = jnp.minimum(place, seq_count - 1 - place)
    KEY, VALUE, QUERY, OUT = range(4)

    def rows_of(slot):
        return pl.ds(pl.multiple_of(slot * own_rows, own_rows), own_rows)

    def block_rows(origin):
        return pl.ds(pl.multiple_of(origin * token_count, token_count), token_count)

    own_rows_at = rows_of(place * dp_count + index)
    loads = [
        pltpu.make_async_copy(
            qkv_hbm.at[pl.ds(1, 2)], weights.at[pl.ds(0, 2), own_rows_at, :], load_sem.at[0]
        ),
        pltpu.make_async_copy(qkv_hbm.at[0], weights.at[QUERY, own_rows_at, :], load_sem.at[1]),
        pltpu.make_async_copy(outw_hbm, weights.at[OUT, own_rows_at, :], load_sem.at[2]),
        pltpu.make_async_copy(tokens_hbm, tok, load_sem.at[3]),
        pltpu.make_async_copy(cotangent_hbm, cot, load_sem.at[4]),
    ]
    for load in loads:
        load.start()

    barrier = pltpu.get_barrier_semaphore()

    def signal(device):
        pl.semaphore_signal(barrier, inc=1, device_id=device, device_id_type=MESH_ID)

    def greet():
        @pl.when(not_first)
        def _():
            signal({"seq": place - 1})

        @pl.when(not_last)
        def _():
            signal({"seq": place + 1})

        for step in range(1, chip_count):
            signal({"dp": (chip + step) % chip_count * CORES + core})
        signal({"dp": chip * CORES + 1 - core})
        for step in range(1, tensor_count):
            signal({"tensor": (lane + step) % tensor_count})
        ends = jnp.minimum(place, 1) + jnp.minimum(seq_count - 1 - place, 1)
        pl.semaphore_wait(barrier, chip_count + tensor_count - 1 + ends)

    greet()

    def remote(source, target, send_sem, recv_sem, device):
        return pltpu.make_async_remote_copy(
            src_ref=source,
            dst_ref=target,
            send_sem=send_sem,
            recv_sem=recv_sem,
            device_id=device,
            device_id_type=MESH_ID,
        )

    up, down = {"seq": place + 1}, {"seq": place - 1}
    beside_device = {"dp": chip * CORES + 1 - core}

    def chip_device(step):
        return {"dp": (chip + step) % chip_count * CORES + core}

    def origin_at(k):
        near = jnp.where(k % 2 == 1, place - (k + 1) // 2, place + k // 2)
        far = jnp.where(
            place * 2 > seq_count - 1, place - (k - both_sides), place + (k - both_sides)
        )
        return jnp.where(k <= 2 * both_sides, near, far)

    event_count = 2 * (seq_count - 1)

    def event(number):
        group, rest = number // 4, number % 4
        if 2 * group + 2 <= seq_count - 1:
            paired = both_sides > group
            piece = jnp.where(paired, rest // 2, rest % 2)
            k = 2 * group + 1 + jnp.where(paired, rest % 2, rest // 2)
        else:
            piece, k = rest % 2, 2 * group + 1 + rest // 2
        return piece, origin_at(k)

    def events_until(k):
        return min(event_count, 4 * ((k + 1) // 2))

    def w_copy(piece, slot, send_sem, device):
        ref = weights.at[piece, rows_of(slot), :]
        return remote(ref, ref, send_sem, w_recv.at[piece, slot], device)

    def w_side(piece, origin, rightward):
        if rightward:
            return w_copy(piece, origin * dp_count + index, w_right.at[piece, origin], up)
        return w_copy(piece, origin * dp_count + index, w_left.at[piece, origin], down)

    def w_across(piece, origin, step):
        sem = w_chip.at[piece, origin * chip_count + step]
        return w_copy(piece, origin * dp_count + index, sem, chip_device(step))

    def w_beside(piece, origin, source_chip):
        sem = w_core.at[piece, origin * chip_count + source_chip]
        return w_copy(piece, origin * dp_count + source_chip * CORES + core, sem, beside_device)

    def w_landed(piece, slot):
        w_copy(piece, slot, w_core.at[piece, 0], beside_device).wait_recv()

    def w_sides_own(first):
        for piece in (first, first + 1):

            @pl.when(not_last)
            def _():
                w_side(piece, place, True).start()

            @pl.when(not_first)
            def _():
                w_side(piece, place, False).start()

    def w_spread_own(first):
        for piece in (first, first + 1):
            for step in range(1, chip_count):
                w_across(piece, place, step).start()
        for piece in (first, first + 1):
            w_beside(piece, place, chip).start()

    def w_step(first, number):
        piece, origin = event(number)
        piece = piece + first
        w_landed(piece, origin * dp_count + index)

        @pl.when((origin < place) & not_last)
        def _():
            w_side(piece, origin, True).start()

        @pl.when((origin > place) & not_first)
        def _():
            w_side(piece, origin, False).start()

        for step in range(1, chip_count):
            w_across(piece, origin, step).start()
        w_beside(piece, origin, chip).start()

    def w_chip_step(first, number):
        piece, origin = (number, place) if number < 2 else event(number - 2)
        piece = piece + first
        for step in range(1, chip_count):
            source_chip = (chip + step) % chip_count
            w_landed(piece, origin * dp_count + source_chip * CORES + core)
            w_beside(piece, origin, source_chip).start()

    def project(first, k):
        origin = origin_at(k)
        rows = pl.ds(pl.multiple_of(origin * plane, plane), plane)
        for piece in (first, first + 1):
            for source_chip in range(chip_count):
                w_landed(piece, origin * dp_count + source_chip * CORES + 1 - core)
        for piece in (first, first + 1):
            source = cot if piece == OUT else unit_low
            product = dot(source[:, rows], weights[piece, rows, :])
            if k == 0:
                acc[piece] = product
            else:
                acc[piece] += product

    def p_copy(piece, origin, rightward):
        ref = pairs.at[piece, block_rows(origin), :]
        if rightward:
            return remote(ref, ref, p_right.at[piece, origin], p_recv.at[piece, origin], up)
        return remote(ref, ref, p_left.at[piece, origin], p_recv.at[piece, origin], down)

    def p_step(number):
        piece, origin = event(number)
        p_copy(piece, origin, True).wait_recv()

        @pl.when((origin < place) & not_last)
        def _():
            p_copy(piece, origin, True).start()

        @pl.when((origin > place) & not_first)
        def _():
            p_copy(piece, origin, False).start()

    def p_sides_own():
        for piece in range(2):

            @pl.when(not_last)
            def _():
                p_copy(piece, place, True).start()

            @pl.when(not_first)
            def _():
                p_copy(piece, place, False).start()

    def normalize_tokens():
        @pl.loop(0, token_count // 32)
        def _(step):
            rows = pl.ds(pl.multiple_of(step * 32, 32), 32)
            values = tok[rows, :].astype(F32)
            average = jnp.mean(values, axis=-1, keepdims=True)
            centered = values - average
            inverse = lax.rsqrt(jnp.mean(centered * centered, axis=-1, keepdims=True) + EPSILON)
            unit_low[rows, :] = (centered * inverse).astype(BF16)
            stat_mean[rows, :] = jnp.broadcast_to(average, (32, 128))
            stat_inv[rows, :] = jnp.broadcast_to(inverse, (32, 128))

    def flip(source, target):
        @pl.loop(0, feature_count // 128)
        def _(step):
            cut = pl.ds(pl.multiple_of(step * 128, 128), 128)
            target[cut, :] = source[:, cut].T

    def key_ready():
        own_block = block_rows(place)
        for h in range(head_count):
            cut = slice(h * HD, (h + 1) * HD)
            normed, inverse = normalize(acc[KEY, :, cut])
            key_unit[:, cut] = normed
            key_inv[:, cut] = jnp.broadcast_to(inverse, (token_count, HD))
            pairs[0, own_block, cut] = normed.astype(BF16)
            pairs[1, own_block, cut] = acc[VALUE, :, cut].astype(BF16)

    def query_ready():
        for h in range(head_count):
            cut = slice(h * HD, (h + 1) * HD)
            normed, inverse = normalize(acc[QUERY, :, cut])
            query_unit[:, cut] = normed
            query_inv[:, cut] = jnp.broadcast_to(inverse, (token_count, HD))
            query_low[:, cut] = normed.astype(BF16)
        grad_low[...] = acc[OUT].astype(BF16)

    loads[0].wait()
    w_sides_own(KEY)
    w_spread_own(KEY)
    for load in loads[1:]:
        load.wait()
    normalize_tokens()

    chip_events = event_count + 2
    at_end = both_sides == 0
    early = min(4, event_count) - 1
    done = 0
    for number in range(event_count):
        w_step(KEY, number)
        if number == early:

            @pl.when(at_end)
            def _():
                w_sides_own(QUERY)

        if number == event_count - 1:

            @pl.when(jnp.logical_not(at_end))
            def _():
                w_sides_own(QUERY)

            w_spread_own(QUERY)
        if number >= 2:
            w_chip_step(KEY, done)
            done += 1
    planes = 0
    passed = 0
    while done < chip_events:
        if chip_events - done <= 2 and passed < min(2, event_count):
            w_step(QUERY, passed)
            passed += 1
        w_chip_step(KEY, done)
        done += 1
        while planes < seq_count - 1 and 2 + events_until(planes) <= done:
            project(KEY, planes)
            planes += 1
    while planes < seq_count:
        project(KEY, planes)
        planes += 1
    key_ready()
    while passed < event_count:
        w_step(QUERY, passed)
        passed += 1
    p_sides_own()
    flip(unit_low, unit_t)
    flip(cot, cot_t)
    done, planes, moved = 0, 0, 0
    while done < chip_events:
        left = chip_events - done
        if left <= 3:
            for _ in range(2 if left == 2 else 1):
                if moved < event_count:
                    p_step(moved)
                    moved += 1
        w_chip_step(QUERY, done)
        done += 1
        while planes < seq_count and 2 + events_until(planes) <= done:
            project(QUERY, planes)
            planes += 1
    query_ready()

    def head_cut(h):
        return pl.ds(pl.multiple_of(h * HD, HD), HD)

    def expo_at(origin, h):
        row = (h * seq_count + origin) * token_count
        return pl.ds(pl.multiple_of(row, token_count), token_count)

    def attend(k):
        origin = origin_at(k)

        @pl.loop(0, head_count)
        def _(h):
            cut = head_cut(h)
            rows = block_rows(origin)
            scores = dot_nt(query_low[:, cut], pairs[0, rows, cut]) * scale
            exponent = jnp.exp(scores)
            low = exponent.astype(BF16)
            expo[expo_at(origin, h), :] = low
            total = exponent[:, :HD]
            for at in range(HD, token_count, HD):
                total = total + exponent[:, at : at + HD]
            mixed = dot(low, pairs[1, rows, cut])
            if k == 0:
                totals[h] = total
                weighted[:, cut] = mixed
            else:
                totals[h] += total
                weighted[:, cut] += mixed

    def attend_end():
        for h in range(head_count):
            cut = slice(h * HD, (h + 1) * HD)
            total = jnp.sum(totals[h], axis=-1, keepdims=True)
            low = (weighted[:, cut] / total).astype(BF16)
            attended[:, cut] = low
            both = grad_low[:, cut].astype(F32) * low.astype(F32)
            totals[h] = jnp.broadcast_to(1.0 / total, (token_count, HD))
            deltas[h] = jnp.broadcast_to(jnp.sum(both, axis=-1, keepdims=True), (token_count, HD))

    for k in range(seq_count):
        while moved < events_until(k):
            p_step(moved)
            moved += 1
        attend(k)
    attend_end()

    def target_at(n):
        return origin_at(seq_count - 1 - n)

    def from_above(target, receiver):
        return jnp.where(target == receiver, seq_count, target)

    def add_into(ref, piece, slot, others, size):
        @pl.loop(0, size // 16)
        def _(step):
            def cut(at):
                return pl.ds(pl.multiple_of(at * size + step * 16, 16), 16)

            total = ref[piece, cut(slot), :].astype(F32)
            for other, at in others:
                total = total + other[piece, cut(at), :].astype(F32)
            ref[piece, cut(slot), :] = total.astype(BF16)

    def g_copy(piece, target, rightward):
        rows = block_rows(target)
        source = part.at[piece, rows, :]
        if rightward:
            into, sem, device = rows, g_low, up
        else:
            into, sem, device = block_rows(from_above(target, place - 1)), g_high, down
        into = part_in.at[piece, into, :]
        return remote(source, into, g_send.at[piece, target], sem.at[piece, target], device)

    def backward(n):
        target = target_at(n)

        @pl.loop(0, head_count)
        def _(h):
            cut = head_cut(h)
            rows = block_rows(target)
            inv_total = totals[h][:, :1]
            probability = expo[expo_at(target, h), :].astype(F32) * inv_total
            gradient = grad_low[:, cut]
            prob_grad = dot_nt(gradient, pairs[1, rows, cut])
            score = (probability * (prob_grad - deltas[h][:, :1]) * scale).astype(BF16)
            query_part = dot(score, pairs[0, rows, cut])
            part[0, rows, cut] = dot_tn(score, query_low[:, cut]).astype(BF16)
            part[1, rows, cut] = dot_tn(probability.astype(BF16), gradient).astype(BF16)
            if n == 0:
                query_raw[:, cut] = query_part
            else:
                query_raw[:, cut] += query_part

    def g_first(piece, n):
        target = target_at(n)

        @pl.when((target > place) & (place == 0))
        def _():
            g_copy(piece, target, True).start()

        @pl.when((target < place) & (place == seq_count - 1))
        def _():
            g_copy(piece, target, False).start()

    def g_step(piece, n):
        target = target_at(n)

        @pl.when((place < target) & not_first)
        def _():
            g_copy(piece, target, True).wait_recv()
            add_into(part, piece, target, [(part_in, target)], token_count)
            g_copy(piece, target, True).start()

        @pl.when((place > target) & not_last)
        def _():
            g_copy(piece, target, False).wait_recv()
            add_into(part, piece, target, [(part_in, target)], token_count)
            g_copy(piece, target, False).start()

    def g_own(piece):
        @pl.when(not_first)
        def _():
            g_copy(piece, place, True).wait_recv()
            add_into(part, piece, place, [(part_in, place)], token_count)

        @pl.when(not_last)
        def _():
            g_copy(piece, place, False).wait_recv()
            add_into(part, piece, place, [(part_in, seq_count)], token_count)

    def back_query():
        for h in range(head_count):
            cut = slice(h * HD, (h + 1) * HD)
            raised = normalize_back(query_raw[:, cut], query_unit[:, cut], query_inv[:, cut])
            back[QUERY, :, cut] = raised.astype(BF16)

    def back_keys():
        own_block = block_rows(place)
        for h in range(head_count):
            cut = slice(h * HD, (h + 1) * HD)
            raw = part[0, own_block, cut].astype(F32)
            raised = normalize_back(raw, key_unit[:, cut], key_inv[:, cut])
            back[KEY, :, cut] = raised.astype(BF16)

    def back_values():
        back[VALUE] = part[1, block_rows(place), :]

    def t_beside(piece, target, target_chip):
        slot = target * chip_count + target_chip
        source = terms.at[piece, rows_of(target * dp_count + target_chip * CORES + 1 - core), :]
        into = held.at[piece, rows_of(slot), :]
        sems = t_core_send.at[piece, slot], t_core_recv.at[piece, slot]
        return remote(source, into, *sems, beside_device)

    def t_across(piece, target, step):
        other = (chip + step) % chip_count
        slot = (step - 1) * seq_count + target
        source = held.at[piece, rows_of(target * chip_count + other), :]
        into = chip_in.at[piece, rows_of(slot), :]
        sems = t_chip_send.at[piece, slot], t_chip_recv.at[piece, slot]
        return remote(source, into, *sems, chip_device(step))

    def t_chain(piece, target, rightward):
        source = held.at[piece, rows_of(target * chip_count + chip), :]
        if rightward:
            at, sem, device = target, t_low_recv, up
        else:
            at, sem, device = from_above(target, place - 1), t_high_recv, down
        into = chain_in.at[piece, rows_of(at), :]
        return remote(source, into, t_chain_send.at[piece, target], sem.at[piece, target], device)

    def make_terms(piece, n):
        target = target_at(n)
        source = cot_t if piece == OUT else unit_t

        right = attended[...] if piece == OUT else back[piece]
        size = plane // CORES
        for at in range(CORES):
            rows = pl.ds(pl.multiple_of(target * plane + at * size, size), size)
            terms[piece, rows, :] = dot(source[rows, :], right).astype(BF16)

        for step in range(1, chip_count):
            t_beside(piece, target, (chip + step) % chip_count).start()
        t_beside(piece, target, chip).start()

    def send_across(piece, n):
        target = target_at(n)
        for step in range(1, chip_count):
            other = (chip + step) % chip_count
            t_beside(piece, target, other).wait_recv()
            own = target * dp_count + other * CORES + core
            add_into(held, piece, target * chip_count + other, [(terms, own)], own_rows)
            t_across(piece, target, step).start()

    def terms_out(piece):
        for n in range(seq_count):
            make_terms(piece, n)
            if n > 0:
                send_across(piece, n - 1)
        send_across(piece, seq_count - 1)

    def gather_y(piece, n):
        target = target_at(n)
        t_beside(piece, target, chip).wait_recv()
        others = [(terms, target * dp_count + index)]
        for step in range(1, chip_count):
            t_across(piece, target, step).wait_recv()
            others.append((chip_in, (step - 1) * seq_count + target))
        add_into(held, piece, target * chip_count + chip, others, own_rows)

        @pl.when((target > place) & (place == 0))
        def _():
            t_chain(piece, target, True).start()

        @pl.when((target < place) & (place == seq_count - 1))
        def _():
            t_chain(piece, target, False).start()

    def pass_z(piece, n):
        target = target_at(n)
        slot = target * chip_count + chip

        @pl.when((place < target) & not_first)
        def _():
            t_chain(piece, target, True).wait_recv()
            add_into(held, piece, slot, [(chain_in, target)], own_rows)
            t_chain(piece, target, True).start()

        @pl.when((place > target) & not_last)
        def _():
            t_chain(piece, target, False).wait_recv()
            add_into(held, piece, slot, [(chain_in, target)], own_rows)
            t_chain(piece, target, False).start()

    width = next(size for size in (512, 384, 256, 128) if share % size == 0)

    def lanes(values):
        total = values[:, :128]
        for at in range(128, width, 128):
            total = total + values[:, at : at + 128]
        return total

    def x_copy(step):
        other = (lane + step) % tensor_count
        sems = x_send.at[step - 1], x_recv.at[step - 1]
        return remote(inner.at[other], inner_in.at[step - 1], *sems, {"tensor": other})

    def xs_copy(step):
        other = (lane + step) % tensor_count
        sems = xs_send.at[step - 1], xs_recv.at[step - 1]
        return remote(sum_rows, sum_rows_in.at[step - 1], *sems, {"tensor": other})

    def inner_grad():
        sums[...] = jnp.zeros_like(sums)

        def tile(owner, step):
            start = owner * share + step * width
            cut = pl.ds(pl.multiple_of(start, width), width)
            product = dot_nt(back[QUERY], weights[QUERY, cut, :])
            product = product + dot_nt(back[KEY], weights[KEY, cut, :])
            product = product + dot_nt(back[VALUE], weights[VALUE, cut, :])
            unit = (tok[:, cut].astype(F32) - stat_mean[:, :1]) * stat_inv[:, :1]
            sums[0] += lanes(product)
            sums[1] += lanes(product * unit)
            at = pl.ds(pl.multiple_of(step * width, width), width)
            inner[owner, :, at] = product.astype(BF16)

        for turn in range(1, tensor_count + 1):

            @pl.loop(0, share // width)
            def _(step):
                tile((lane + turn) % tensor_count, step)

            if turn < tensor_count:
                x_copy(turn).start()
        sum_rows[...] = jnp.zeros_like(sum_rows)
        for at in range(2):
            sum_rows[at : at + 1, :] = jnp.sum(sums[at].T, axis=0, keepdims=True)
        for step in range(1, tensor_count):
            xs_copy(step).start()

    def finish_branch():
        for step in range(1, tensor_count):
            x_copy(step).wait_recv()
            xs_copy(step).wait_recv()
        total = sum_rows[...]
        for other in range(tensor_count - 1):
            total = total + sum_rows_in[other]
        sum_columns[...] = total.T / feature_count

        @pl.loop(0, token_count // 16)
        def _(step):
            rows = pl.ds(pl.multiple_of(step * 16, 16), 16)
            values = inner[lane, rows, :].astype(F32)
            for other in range(tensor_count - 1):
                values = values + inner_in[other, rows, :].astype(F32)
            means = sum_columns[rows, :]
            mean_grad, mean_both = means[:, 0:1], means[:, 1:2]
            cut = pl.ds(pl.multiple_of(lane * share, share), share)
            inverse = stat_inv[rows, :][:, :1]
            unit = (tok[rows, cut].astype(F32) - stat_mean[rows, :][:, :1]) * inverse
            branch_out[rows, :] = ((values - mean_grad - unit * mean_both) * inverse).astype(BF16)

    def finish_weights(piece):
        own_held = place * chip_count + chip

        @pl.when(not_first)
        def _():
            t_chain(piece, place, True).wait_recv()

        @pl.when(not_last)
        def _():
            t_chain(piece, place, False).wait_recv()

        @pl.loop(0, own_rows // 16)
        def _(step):
            rows = pl.ds(pl.multiple_of(step * 16, 16), 16)

            def cut(at):
                return pl.ds(pl.multiple_of(at * own_rows + step * 16, 16), 16)

            summed[piece, rows, :] = held[piece, cut(own_held), :].astype(F32)

            @pl.when(not_first)
            def _():
                summed[piece, rows, :] += chain_in[piece, cut(place), :].astype(F32)

            @pl.when(not_last)
            def _():
                summed[piece, rows, :] += chain_in[piece, cut(seq_count), :].astype(F32)

    def out_copy(piece):
        target = outw_out if piece == OUT else qkv_out.at[(1, 2, 0)[piece]]
        return pltpu.make_async_copy(summed.at[piece], target, store_sem.at[piece])

    def branch_copy():
        return pltpu.make_async_copy(branch_out, branch_hbm, store_sem.at[4])

    for n in range(seq_count):
        backward(n)
        g_first(0, n)
        if n == min(1, seq_count - 1):
            terms_out(OUT)
    for n in range(seq_count):
        g_first(1, n)
    back_query()
    terms_out(QUERY)
    for n in range(seq_count):
        gather_y(OUT, n)
    for n in range(seq_count - 1):
        g_step(0, n)
    g_own(0)
    back_keys()
    terms_out(KEY)
    for n in range(seq_count - 1):
        g_step(1, n)
    g_own(1)
    back_values()
    terms_out(VALUE)
    for n in range(seq_count):
        gather_y(QUERY, n)
    pass_z(OUT, 0)
    inner_grad()
    for n in range(1, seq_count - 1):
        pass_z(OUT, n)
    for n in range(seq_count):
        gather_y(KEY, n)
        if n < seq_count - 1:
            pass_z(QUERY, n)
    for n in range(seq_count):
        gather_y(VALUE, n)
        if n < seq_count - 1:
            pass_z(KEY, n)
    for n in range(seq_count - 1):
        pass_z(VALUE, n)
    for piece in (OUT, QUERY, KEY):
        finish_weights(piece)
        out_copy(piece).start()
    finish_branch()
    branch_copy().start()
    finish_weights(VALUE)
    out_copy(VALUE).start()
    for piece in range(4):
        out_copy(piece).wait()
    branch_copy().wait()

    def drain():
        for origin in range(seq_count):
            to_right = (origin <= place) & not_last
            to_left = (origin >= place) & not_first
            for piece in range(4):
                for step in range(1, chip_count):
                    w_across(piece, origin, step).wait_send()
                    t_across(piece, origin, step).wait_send()
                for source_chip in range(chip_count):
                    w_beside(piece, origin, source_chip).wait_send()
                    t_beside(piece, origin, source_chip).wait_send()

                @pl.when(to_right)
                def _():
                    w_side(piece, origin, True).wait_send()

                @pl.when(to_left)
                def _():
                    w_side(piece, origin, False).wait_send()

                @pl.when(place != origin)
                def _():
                    t_chain(piece, origin, True).wait_send()

            for piece in range(2):

                @pl.when(to_right)
                def _():
                    p_copy(piece, origin, True).wait_send()

                @pl.when(to_left)
                def _():
                    p_copy(piece, origin, False).wait_send()

                @pl.when(place != origin)
                def _():
                    g_copy(piece, origin, True).wait_send()

        for step in range(1, tensor_count):
            x_copy(step).wait_send()
            xs_copy(step).wait_send()

    drain()


def local(tokens, cotangent, qkv_weight, out_weight):
    seq_count, dp_count = lax.axis_size("seq"), lax.axis_size("dp")
    tensor_count = lax.axis_size("tensor")
    chip_count = dp_count // CORES
    row_count, feature_count = tokens.shape[1:]
    own_rows, columns = out_weight.shape
    head_count = columns // HD
    share = feature_count // tensor_count
    sizes = (seq_count, dp_count, tensor_count, own_rows, head_count)

    def vmem(*shape, kind=BF16):
        return pltpu.VMEM(shape, kind)

    def dma(*shape):
        return pltpu.SemaphoreType.DMA(shape)

    both, peers = seq_count * chip_count, seq_count * max(chip_count - 1, 1)
    others = max(tensor_count - 1, 1)
    scratch = [
        vmem(row_count, feature_count),
        vmem(row_count, feature_count),
        vmem(row_count, feature_count),
        vmem(feature_count, row_count),
        vmem(feature_count, row_count),
        vmem(row_count, 128, kind=F32),
        vmem(row_count, 128, kind=F32),
        vmem(4, feature_count, columns),
        vmem(4, row_count, columns, kind=F32),
        vmem(2, seq_count * row_count, columns),
        vmem(row_count, columns),
        vmem(row_count, columns, kind=F32),
        vmem(row_count, columns, kind=F32),
        vmem(row_count, columns, kind=F32),
        vmem(row_count, columns, kind=F32),
        vmem(row_count, columns),
        vmem(head_count * seq_count * row_count, row_count),
        vmem(head_count, row_count, HD, kind=F32),
        vmem(head_count, row_count, HD, kind=F32),
        vmem(row_count, columns, kind=F32),
        vmem(row_count, columns),
        vmem(row_count, columns, kind=F32),
        vmem(2, seq_count * row_count, columns),
        vmem(2, (seq_count + 1) * row_count, columns),
        vmem(3, row_count, columns),
        vmem(tensor_count, row_count, share),
        vmem(others, row_count, share),
        vmem(2, row_count, 128, kind=F32),
        vmem(4, feature_count, columns),
        vmem(4, both * own_rows, columns),
        vmem(4, peers * own_rows, columns),
        vmem(4, (seq_count + 1) * own_rows, columns),
        vmem(4, own_rows, columns, kind=F32),
        vmem(row_count, share),
        vmem(8, row_count, kind=F32),
        vmem(others, 8, row_count, kind=F32),
        vmem(row_count, 8, kind=F32),
        dma(5),
        dma(5),
        dma(4, seq_count * dp_count),
        dma(4, seq_count),
        dma(4, seq_count),
        dma(4, both),
        dma(4, both),
        dma(2, seq_count),
        dma(2, seq_count),
        dma(2, seq_count),
        dma(2, seq_count),
        dma(2, seq_count),
        dma(2, seq_count),
        dma(4, both),
        dma(4, both),
        dma(4, peers),
        dma(4, peers),
        dma(4, seq_count),
        dma(4, seq_count),
        dma(4, seq_count),
        dma(others),
        dma(others),
        dma(others),
        dma(others),
    ]
    anywhere = pl.BlockSpec(memory_space=pl.ANY)
    qkv_grad, out_grad, branch = pl.pallas_call(
        functools.partial(body, sizes),
        out_shape=(
            jax.ShapeDtypeStruct((3, own_rows, columns), F32),
            jax.ShapeDtypeStruct((own_rows, columns), F32),
            jax.ShapeDtypeStruct((row_count, share), BF16),
        ),
        in_specs=[anywhere] * 4,
        out_specs=(anywhere, anywhere, anywhere),
        scratch_shapes=scratch,
        compiler_params=pltpu.CompilerParams(
            collective_id=0, has_side_effects=True, vmem_limit_bytes=67043328
        ),
        name="layer",
    )(tokens[0], cotangent[0], jnp.transpose(qkv_weight, (1, 0, 2)), out_weight)
    return jnp.transpose(qkv_grad, (1, 0, 2)), out_grad, branch[None]


def solution(mesh):
    return jax.shard_map(
        local,
        mesh=mesh,
        in_specs=(
            P("dp", "seq", None),
            P("dp", "seq", None),
            P(("seq", "dp"), None, "tensor"),
            P(("seq", "dp"), "tensor"),
        ),
        out_specs=(
            P(("seq", "dp"), None, "tensor"),
            P(("seq", "dp"), "tensor"),
            P("dp", "seq", "tensor"),
        ),
        check_vma=False,
    )
```

time: 174 us -> 160 us (0.920)
  Pallas kernels: 169 us -> 155 us
    pallas_call x1, Pallas kernels: 169 us -> 155 us  [local(): pl.pallas_call(functools.partial(body, sizes), out_shape=(jax.ShapeDtypeS...]
where the time goes in v2:
time: 160 us
  Pallas kernels  155 us (97%)
  local copies, waits for them, and re-layouts  3.83 us (2%)
    pallas_call x1, Pallas kernels, local(): pl.pallas_call(functools.partial(body, sizes), out_shape=(jax.ShapeDtypeS...  155 us
    unnamed x7, local copies, waits for them, and re-layouts  3.83 us

profile of v2, /device:TPU:0, one launch (start us, length us, event | category | flops | bytes accessed | tf_op | source)
XLA Modules:
  0.0 159.8 jit_solution(4110397498726170845)
XLA Ops:
  0.6 155.3 %layer.1 = (f32[3,192,384]{2,1,0:T(8,128)}, f32[192,384]{1,0:T(8,128)}, bf16[256,1536]{1,0:T(8,128)(2,1)}) custom-call(bf16[256,3072]{1,0:T(8,128)(2,1)} %bitcast.5, bf16[256,3072]{1,0:T(8,128)(2,1)} %bitcast.6, bf16[3,192,384]{2,1,0:T(8,128)(2,1)} %bitcast.9, bf16[192,384]{1,0:T(8,128)(2,1)} %outw_hbm.1), custom_call_target="tpu_custom_call" | custom-call | tf_op jit(solution)/shard_map/layer/pallas_call | solution.py:928
  155.9 0.0 copy-start.1
  155.9 0.0 copy-start
  156.0 2.2 %copy.10 = f32[192,3,384]{2,0,1:T(8,128)} copy(f32[192,3,384]{2,0,1:T(8,128)} %bitcast.7) | data formatting | bytes 1769472
  158.2 0.0 copy-done.1
  158.2 0.7 copy.11
  158.9 0.0 copy-done
  158.9 0.9 copy.12
Async XLA Ops:
  155.9 2.2 %copy-start.1 = (f32[192,384]{1,0:T(8,128)S(1)}, f32[192,384]{1,0:T(8,128)}, u32[]{:S(2)}) copy-start(f32[192,384]{1,0:T(8,128)} %get-tuple-element.13) | copy-start | bytes 884740
  155.9 3.0 %copy-start = (bf16[256,1536]{1,0:T(8,128)(2,1)S(1)}, bf16[256,1536]{1,0:T(8,128)(2,1)}, u32[]{:S(2)}) copy-start(bf16[256,1536]{1,0:T(8,128)(2,1)} %get-tuple-element.8) | copy-start | bytes 2359300

commit v3 on v2

--- a/solution.py
+++ b/solution.py
@@ -12,6 +12,193 @@
 MESH_ID = pl.DeviceIdType.MESH
 EPSILON = 1e-06
 F32, BF16 = jnp.float32, jnp.bfloat16
+
+
+(
+    W_KV,
+    OWN_QUERY,
+    SPREAD_QUERY,
+    CHIP_KV,
+    MIX_KV,
+    KEY_READY,
+    W_QO,
+    SEND_PAIRS,
+    FLIP_UNIT,
+    FLIP_COT,
+    CHIP_QO,
+    MIX_QO,
+    PAIR,
+    QUERY_READY,
+    ATTEND,
+    ATTEND_END,
+    BACKWARD,
+    FIRST_KEY,
+    FIRST_VALUE,
+    MAKE_OUT,
+    ACROSS_OUT,
+    BACK_QUERY,
+    MAKE_QUERY,
+    ACROSS_QUERY,
+    Y_OUT,
+    G_KEY,
+    OWN_KEY,
+    BACK_KEYS,
+    MAKE_KEY,
+    ACROSS_KEY,
+    G_VALUE,
+    OWN_VALUE,
+    BACK_VALUES,
+    MAKE_VALUE,
+    ACROSS_VALUE,
+    Y_QUERY,
+    Z_OUT,
+    INNER_GRAD,
+    Y_KEY,
+    Z_QUERY,
+    Y_VALUE,
+    Z_KEY,
+    Z_VALUE,
+    FINISH_OUT,
+    FINISH_QUERY,
+    FINISH_KEY,
+    FINISH_BRANCH,
+    FINISH_VALUE,
+) = range(48)
+FORWARD_TIMES = {
+    W_KV: (-4.87, 5.57),
+    OWN_QUERY: (-12.55, 3.56),
+    SPREAD_QUERY: (27.94, 1.11),
+    CHIP_KV: (11.34, 3.56),
+    MIX_KV: (29.29, 1.26),
+    KEY_READY: (20.32, 0.0),
+    W_QO: (26.16, 3.27),
+    SEND_PAIRS: (26.3, 0.47),
+    FLIP_UNIT: (52.59, 0.0),
+    FLIP_COT: (19.92, 1.65),
+    CHIP_QO: (37.05, 3.63),
+    MIX_QO: (34.13, 6.34),
+    PAIR: (42.23, 6.16),
+    QUERY_READY: (67.43, 6.51),
+    ATTEND: (45.34, 0.0),
+    ATTEND_END: (77.44, 0.0),
+}
+BACKWARD_TIMES = {
+    BACKWARD: (-2.19, 2.64),
+    FIRST_KEY: (-2.46, 1.91),
+    FIRST_VALUE: (6.2, 0.54),
+    MAKE_OUT: (1.52, 0.0),
+    ACROSS_OUT: (4.71, 0.17),
+    BACK_QUERY: (2.54, 0.0),
+    MAKE_QUERY: (-18.11, 0.64),
+    ACROSS_QUERY: (15.9, 0.82),
+    Y_OUT: (18.34, 0.0),
+    G_KEY: (3.85, 0.0),
+    OWN_KEY: (18.05, 1.39),
+    BACK_KEYS: (29.33, 0.5),
+    MAKE_KEY: (2.07, 0.03),
+    ACROSS_KEY: (9.4, 2.81),
+    G_VALUE: (21.95, 2.42),
+    OWN_VALUE: (32.26, 0.0),
+    BACK_VALUES: (47.91, 1.68),
+    MAKE_VALUE: (15.23, 0.0),
+    ACROSS_VALUE: (45.49, 1.78),
+    Y_QUERY: (38.62, 4.26),
+    Z_OUT: (30.05, 5.94),
+    INNER_GRAD: (52.42, 4.91),
+    Y_KEY: (46.6, 6.84),
+    Z_QUERY: (51.97, 0.56),
+    Y_VALUE: (59.28, 0.83),
+    Z_KEY: (53.48, 2.55),
+    Z_VALUE: (65.73, 6.14),
+    FINISH_OUT: (83.86, 0.52),
+    FINISH_QUERY: (68.47, 0.33),
+    FINISH_KEY: (78.69, 2.43),
+    FINISH_BRANCH: (89.16, 1.92),
+    FINISH_VALUE: (92.27, 0.0),
+}
+
+
+PIECES = (
+    (BACK_KEYS, MAKE_KEY, ACROSS_KEY, Y_KEY, Z_KEY, FINISH_KEY),
+    (BACK_VALUES, MAKE_VALUE, ACROSS_VALUE, Y_VALUE, Z_VALUE, FINISH_VALUE),
+    (BACK_QUERY, MAKE_QUERY, ACROSS_QUERY, Y_QUERY, Z_QUERY, FINISH_QUERY),
+    (None, MAKE_OUT, ACROSS_OUT, Y_OUT, Z_OUT, FINISH_OUT),
+)
+
+
+def events_until(k, seq_count):
+    return min(2 * (seq_count - 1), 4 * ((k + 1) // 2))
+
+
+def forward_steps(seq_count):
+    events = 2 * (seq_count - 1)
+    needs = {(OWN_QUERY, 0): [(W_KV, min(4, events) - 1)] if events else [], (SPREAD_QUERY, 0): []}
+    for come, across, mix in ((W_KV, CHIP_KV, MIX_KV), (W_QO, CHIP_QO, MIX_QO)):
+        for n in range(events):
+            needs[come, n] = [(come, n - 1)] if n else []
+        for n in range(events + 2):
+            needs[across, n] = [(across, n - 1)] if n else []
+            if n > 1:
+                needs[across, n].append((come, n - 2))
+        for k in range(seq_count):
+            needs[mix, k] = [(across, 1 + events_until(k, seq_count))]
+            if k:
+                needs[mix, k].append((mix, k - 1))
+    for n in range(2):
+        needs[CHIP_QO, n].append((SPREAD_QUERY, 0))
+    if events:
+        needs[W_QO, 0] = [(OWN_QUERY, 1)]
+    needs[OWN_QUERY, 1] = [(OWN_QUERY, 0)] + ([(W_KV, events - 1)] if events else [])
+    needs[KEY_READY, 0] = [(MIX_KV, seq_count - 1)]
+    needs[SEND_PAIRS, 0] = [(KEY_READY, 0)]
+    needs[FLIP_UNIT, 0] = needs[FLIP_COT, 0] = []
+    for n in range(events):
+        needs[PAIR, n] = [(PAIR, n - 1) if n else (SEND_PAIRS, 0)]
+    needs[QUERY_READY, 0] = [(MIX_QO, seq_count - 1)]
+    for k in range(seq_count):
+        needs[ATTEND, k] = [(ATTEND, k - 1) if k else (QUERY_READY, 0), (KEY_READY, 0)]
+        if events_until(k, seq_count):
+            needs[ATTEND, k].append((PAIR, events_until(k, seq_count) - 1))
+    ends = [(ATTEND, seq_count - 1), (FLIP_UNIT, 0), (FLIP_COT, 0)]
+    needs[ATTEND_END, 0] = ends
+    return in_order(needs, FORWARD_TIMES)
+
+
+def backward_steps(seq_count):
+    needs, last = {}, seq_count - 1
+
+    def chained(name, count, more):
+        for n in range(count):
+            needs[name, n] = ([(name, n - 1)] if n else []) + more(n)
+
+    chained(BACKWARD, seq_count, lambda n: [])
+    for first, come, own in ((FIRST_KEY, G_KEY, OWN_KEY), (FIRST_VALUE, G_VALUE, OWN_VALUE)):
+        chained(first, seq_count, lambda n: [(BACKWARD, n)])
+        chained(come, last, lambda n: [(first, last)])
+        needs[own, 0] = [(come, last - 1) if last else (first, last)]
+    needs[BACK_QUERY, 0] = [(BACKWARD, last)]
+    needs[BACK_KEYS, 0] = [(OWN_KEY, 0)]
+    needs[BACK_VALUES, 0] = [(OWN_VALUE, 0)]
+    for ready, make, across, come, chain, finish in PIECES:
+        first = [] if ready is None else [(ready, 0)]
+        chained(make, seq_count, lambda n: first)
+        chained(across, seq_count, lambda n: [(make, n)])
+        chained(come, seq_count, lambda n: [(across, n)])
+        chained(chain, last, lambda n: [(come, n)])
+        needs[finish, 0] = [(come, last)] + ([(chain, last - 1)] if last else [])
+    needs[INNER_GRAD, 0] = [(BACK_VALUES, 0), (BACK_KEYS, 0), (BACK_QUERY, 0)]
+    needs[FINISH_BRANCH, 0] = [(INNER_GRAD, 0)]
+    return in_order(needs, BACKWARD_TIMES)
+
+
+def in_order(needs, times):
+    left, steps = dict(needs), []
+    while left:
+        able = [step for step in left if not any(other in left for other in left[step])]
+        best = min(able, key=lambda step: (times[step[0]][0] + times[step[0]][1] * step[1], step))
+        steps.append(best)
+        del left[best]
+    return steps
 
 
 def dot(left, right):
@@ -87,21 +274,15 @@
     load_sem,
     store_sem,
     w_recv,
-    w_right,
-    w_left,
-    w_chip,
-    w_core,
+    w_send,
     p_recv,
-    p_right,
-    p_left,
+    p_send,
     g_low,
     g_high,
     g_send,
-    t_core_send,
     t_core_recv,
-    t_chip_send,
     t_chip_recv,
-    t_chain_send,
+    t_send,
     t_low_recv,
     t_high_recv,
     x_send,
@@ -189,8 +370,6 @@
         )
         return jnp.where(k <= 2 * both_sides, near, far)
 
-    event_count = 2 * (seq_count - 1)
-
     def event(number):
         group, rest = number // 4, number % 4
         if 2 * group + 2 <= seq_count - 1:
@@ -201,28 +380,24 @@
             piece, k = rest % 2, 2 * group + 1 + rest // 2
         return piece, origin_at(k)
 
-    def events_until(k):
-        return min(event_count, 4 * ((k + 1) // 2))
-
     def w_copy(piece, slot, send_sem, device):
         ref = weights.at[piece, rows_of(slot), :]
         return remote(ref, ref, send_sem, w_recv.at[piece, slot], device)
 
     def w_side(piece, origin, rightward):
         if rightward:
-            return w_copy(piece, origin * dp_count + index, w_right.at[piece, origin], up)
-        return w_copy(piece, origin * dp_count + index, w_left.at[piece, origin], down)
+            return w_copy(piece, origin * dp_count + index, w_send.at[0], up)
+        return w_copy(piece, origin * dp_count + index, w_send.at[0], down)
 
     def w_across(piece, origin, step):
-        sem = w_chip.at[piece, origin * chip_count + step]
-        return w_copy(piece, origin * dp_count + index, sem, chip_device(step))
+        return w_copy(piece, origin * dp_count + index, w_send.at[1], chip_device(step))
 
     def w_beside(piece, origin, source_chip):
-        sem = w_core.at[piece, origin * chip_count + source_chip]
-        return w_copy(piece, origin * dp_count + source_chip * CORES + core, sem, beside_device)
+        slot = origin * dp_count + source_chip * CORES + core
+        return w_copy(piece, slot, w_send.at[2], beside_device)
 
     def w_landed(piece, slot):
-        w_copy(piece, slot, w_core.at[piece, 0], beside_device).wait_recv()
+        w_copy(piece, slot, w_send.at[2], beside_device).wait_recv()
 
     def w_sides_own(first):
         for piece in (first, first + 1):
@@ -284,8 +459,8 @@
     def p_copy(piece, origin, rightward):
         ref = pairs.at[piece, block_rows(origin), :]
         if rightward:
-            return remote(ref, ref, p_right.at[piece, origin], p_recv.at[piece, origin], up)
-        return remote(ref, ref, p_left.at[piece, origin], p_recv.at[piece, origin], down)
+            return remote(ref, ref, p_send.at[0], p_recv.at[piece, origin], up)
+        return remote(ref, ref, p_send.at[0], p_recv.at[piece, origin], down)
 
     def p_step(number):
         piece, origin = event(number)
@@ -353,64 +528,6 @@
     for load in loads[1:]:
         load.wait()
     normalize_tokens()
-
-    chip_events = event_count + 2
-    at_end = both_sides == 0
-    early = min(4, event_count) - 1
-    done = 0
-    for number in range(event_count):
-        w_step(KEY, number)
-        if number == early:
-
-            @pl.when(at_end)
-            def _():
-                w_sides_own(QUERY)
-
-        if number == event_count - 1:
-
-            @pl.when(jnp.logical_not(at_end))
-            def _():
-                w_sides_own(QUERY)
-
-            w_spread_own(QUERY)
-        if number >= 2:
-            w_chip_step(KEY, done)
-            done += 1
-    planes = 0
-    passed = 0
-    while done < chip_events:
-        if chip_events - done <= 2 and passed < min(2, event_count):
-            w_step(QUERY, passed)
-            passed += 1
-        w_chip_step(KEY, done)
-        done += 1
-        while planes < seq_count - 1 and 2 + events_until(planes) <= done:
-            project(KEY, planes)
-            planes += 1
-    while planes < seq_count:
-        project(KEY, planes)
-        planes += 1
-    key_ready()
-    while passed < event_count:
-        w_step(QUERY, passed)
-        passed += 1
-    p_sides_own()
-    flip(unit_low, unit_t)
-    flip(cot, cot_t)
-    done, planes, moved = 0, 0, 0
-    while done < chip_events:
-        left = chip_events - done
-        if left <= 3:
-            for _ in range(2 if left == 2 else 1):
-                if moved < event_count:
-                    p_step(moved)
-                    moved += 1
-        w_chip_step(QUERY, done)
-        done += 1
-        while planes < seq_count and 2 + events_until(planes) <= done:
-            project(QUERY, planes)
-            planes += 1
-    query_ready()
 
     def head_cut(h):
         return pl.ds(pl.multiple_of(h * HD, HD), HD)
@@ -451,12 +568,33 @@
             totals[h] = jnp.broadcast_to(1.0 / total, (token_count, HD))
             deltas[h] = jnp.broadcast_to(jnp.sum(both, axis=-1, keepdims=True), (token_count, HD))
 
-    for k in range(seq_count):
-        while moved < events_until(k):
-            p_step(moved)
-            moved += 1
-        attend(k)
-    attend_end()
+    at_end = both_sides == 0
+
+    def own_query(number):
+        @pl.when(jnp.logical_not(at_end) if number else at_end)
+        def _():
+            w_sides_own(QUERY)
+
+    ahead = {
+        W_KV: lambda n: w_step(KEY, n),
+        OWN_QUERY: own_query,
+        SPREAD_QUERY: lambda n: w_spread_own(QUERY),
+        CHIP_KV: lambda n: w_chip_step(KEY, n),
+        MIX_KV: lambda n: project(KEY, n),
+        KEY_READY: lambda n: key_ready(),
+        W_QO: lambda n: w_step(QUERY, n),
+        SEND_PAIRS: lambda n: p_sides_own(),
+        FLIP_UNIT: lambda n: flip(unit_low, unit_t),
+        FLIP_COT: lambda n: flip(cot, cot_t),
+        CHIP_QO: lambda n: w_chip_step(QUERY, n),
+        MIX_QO: lambda n: project(QUERY, n),
+        PAIR: p_step,
+        QUERY_READY: lambda n: query_ready(),
+        ATTEND: attend,
+        ATTEND_END: lambda n: attend_end(),
+    }
+    for name, number in forward_steps(seq_count):
+        ahead[name](number)
 
     def target_at(n):
         return origin_at(seq_count - 1 - n)
@@ -483,7 +621,7 @@
         else:
             into, sem, device = block_rows(from_above(target, place - 1)), g_high, down
         into = part_in.at[piece, into, :]
-        return remote(source, into, g_send.at[piece, target], sem.at[piece, target], device)
+        return remote(source, into, g_send.at[0], sem.at[piece, target], device)
 
     def backward(n):
         target = target_at(n)
@@ -563,7 +701,7 @@
         slot = target * chip_count + target_chip
         source = terms.at[piece, rows_of(target * dp_count + target_chip * CORES + 1 - core), :]
         into = held.at[piece, rows_of(slot), :]
-        sems = t_core_send.at[piece, slot], t_core_recv.at[piece, slot]
+        sems = t_send.at[0], t_core_recv.at[piece, slot]
         return remote(source, into, *sems, beside_device)
 
     def t_across(piece, target, step):
@@ -571,7 +709,7 @@
         slot = (step - 1) * seq_count + target
         source = held.at[piece, rows_of(target * chip_count + other), :]
         into = chip_in.at[piece, rows_of(slot), :]
-        sems = t_chip_send.at[piece, slot], t_chip_recv.at[piece, slot]
+        sems = t_send.at[1], t_chip_recv.at[piece, slot]
         return remote(source, into, *sems, chip_device(step))
 
     def t_chain(piece, target, rightward):
@@ -581,7 +719,7 @@
         else:
             at, sem, device = from_above(target, place - 1), t_high_recv, down
         into = chain_in.at[piece, rows_of(at), :]
-        return remote(source, into, t_chain_send.at[piece, target], sem.at[piece, target], device)
+        return remote(source, into, t_send.at[2], sem.at[piece, target], device)
 
     def make_terms(piece, n):
         target = target_at(n)
@@ -605,13 +743,6 @@
             own = target * dp_count + other * CORES + core
             add_into(held, piece, target * chip_count + other, [(terms, own)], own_rows)
             t_across(piece, target, step).start()
-
-    def terms_out(piece):
-        for n in range(seq_count):
-            make_terms(piece, n)
-            if n > 0:
-                send_across(piece, n - 1)
-        send_across(piece, seq_count - 1)
 
     def gather_y(piece, n):
         target = target_at(n)
@@ -750,91 +881,64 @@
     def branch_copy():
         return pltpu.make_async_copy(branch_out, branch_hbm, store_sem.at[4])
 
-    for n in range(seq_count):
-        backward(n)
-        g_first(0, n)
-        if n == min(1, seq_count - 1):
-            terms_out(OUT)
-    for n in range(seq_count):
-        g_first(1, n)
-    back_query()
-    terms_out(QUERY)
-    for n in range(seq_count):
-        gather_y(OUT, n)
-    for n in range(seq_count - 1):
-        g_step(0, n)
-    g_own(0)
-    back_keys()
-    terms_out(KEY)
-    for n in range(seq_count - 1):
-        g_step(1, n)
-    g_own(1)
-    back_values()
-    terms_out(VALUE)
-    for n in range(seq_count):
-        gather_y(QUERY, n)
-    pass_z(OUT, 0)
-    inner_grad()
-    for n in range(1, seq_count - 1):
-        pass_z(OUT, n)
-    for n in range(seq_count):
-        gather_y(KEY, n)
-        if n < seq_count - 1:
-            pass_z(QUERY, n)
-    for n in range(seq_count):
-        gather_y(VALUE, n)
-        if n < seq_count - 1:
-            pass_z(KEY, n)
-    for n in range(seq_count - 1):
-        pass_z(VALUE, n)
-    for piece in (OUT, QUERY, KEY):
+    def finish(piece):
         finish_weights(piece)
         out_copy(piece).start()
-    finish_branch()
-    branch_copy().start()
-    finish_weights(VALUE)
-    out_copy(VALUE).start()
+
+    def branch_end():
+        finish_branch()
+        branch_copy().start()
+
+    behind = {
+        BACKWARD: backward,
+        FIRST_KEY: lambda n: g_first(0, n),
+        FIRST_VALUE: lambda n: g_first(1, n),
+        BACK_QUERY: lambda n: back_query(),
+        G_KEY: lambda n: g_step(0, n),
+        OWN_KEY: lambda n: g_own(0),
+        BACK_KEYS: lambda n: back_keys(),
+        G_VALUE: lambda n: g_step(1, n),
+        OWN_VALUE: lambda n: g_own(1),
+        BACK_VALUES: lambda n: back_values(),
+        INNER_GRAD: lambda n: inner_grad(),
+        FINISH_BRANCH: lambda n: branch_end(),
+    }
+    for piece, (_, make, across, come, chain, end) in enumerate(PIECES):
+        behind[make] = functools.partial(make_terms, piece)
+        behind[across] = functools.partial(send_across, piece)
+        behind[come] = functools.partial(gather_y, piece)
+        behind[chain] = functools.partial(pass_z, piece)
+        behind[end] = lambda n, piece=piece: finish(piece)
+    for name, number in backward_steps(seq_count):
+        behind[name](number)
     for piece in range(4):
         out_copy(piece).wait()
     branch_copy().wait()
 
+    def left(ref, rows, sem):
+        block = ref.at[:, pl.ds(0, rows), :]
+        remote(block, block, sem, w_recv.at[0, 0], beside_device).wait_send()
+
     def drain():
-        for origin in range(seq_count):
-            to_right = (origin <= place) & not_last
-            to_left = (origin >= place) & not_first
-            for piece in range(4):
-                for step in range(1, chip_count):
-                    w_across(piece, origin, step).wait_send()
-                    t_across(piece, origin, step).wait_send()
-                for source_chip in range(chip_count):
-                    w_beside(piece, origin, source_chip).wait_send()
-                    t_beside(piece, origin, source_chip).wait_send()
-
-                @pl.when(to_right)
-                def _():
-                    w_side(piece, origin, True).wait_send()
-
-                @pl.when(to_left)
-                def _():
-                    w_side(piece, origin, False).wait_send()
-
-                @pl.when(place != origin)
-                def _():
-                    t_chain(piece, origin, True).wait_send()
-
-            for piece in range(2):
-
-                @pl.when(to_right)
-                def _():
-                    p_copy(piece, origin, True).wait_send()
-
-                @pl.when(to_left)
-                def _():
-                    p_copy(piece, origin, False).wait_send()
-
-                @pl.when(place != origin)
-                def _():
-                    g_copy(piece, origin, True).wait_send()
+        both, peers = seq_count * chip_count, seq_count * (chip_count - 1)
+        if peers:
+            left(weights, peers * own_rows, w_send.at[1])
+            left(chip_in, peers * own_rows, t_send.at[1])
+        left(weights, both * own_rows, w_send.at[2])
+        left(held, both * own_rows, t_send.at[0])
+        if seq_count > 1:
+            left(chain_in, (seq_count - 1) * own_rows, t_send.at[2])
+            left(part, (seq_count - 1) * token_count, g_send.at[0])
+
+            @pl.when(at_end)
+            def _():
+                left(weights, own_rows, w_send.at[0])
+                left(part_in, token_count, p_send.at[0])
+
+            @pl.when(jnp.logical_not(at_end))
+            def _():
+                left(weights, (seq_count + 1) * own_rows, w_send.at[0])
+                left(part_in, (seq_count + 1) * token_count, p_send.at[0])
 
         for step in range(1, tensor_count):
             x_copy(step).wait_send()
@@ -902,21 +1006,15 @@
         dma(5),
         dma(5),
         dma(4, seq_count * dp_count),
-        dma(4, seq_count),
-        dma(4, seq_count),
-        dma(4, both),
-        dma(4, both),
+        dma(3),
+        dma(2, seq_count),
+        dma(1),
         dma(2, seq_count),
         dma(2, seq_count),
-        dma(2, seq_count),
-        dma(2, seq_count),
-        dma(2, seq_count),
-        dma(2, seq_count),
-        dma(4, both),
+        dma(1),
         dma(4, both),
         dma(4, peers),
-        dma(4, peers),
-        dma(4, seq_count),
+        dma(3),
         dma(4, seq_count),
         dma(4, seq_count),
         dma(others),

time: 160 us -> 144 us (0.900)
  Pallas kernels: 155 us -> 139 us
    pallas_call x1, Pallas kernels: 155 us -> 139 us  [local(): pl.pallas_call(functools.partial(body, sizes), out_shape=(jax.ShapeDtypeS...]
where the time goes in v3:
time: 144 us; the launch traced here: 143 us
  Pallas kernels  139 us (97%)
  local copies, waits for them, and re-layouts  3.83 us (3%)
    pallas_call x1, Pallas kernels, local(): pl.pallas_call(functools.partial(body, sizes), out_shape=(jax.ShapeDtypeS...  139 us
    unnamed x7, local copies, waits for them, and re-layouts  3.83 us

profile of v3, /device:TPU:0, one launch (start us, length us, event | category | flops | bytes accessed | tf_op | source)
XLA Modules:
  0.0 143.5 jit_solution(9441835125607163026)
XLA Ops:
  0.6 139.0 %layer.1 = (f32[3,192,384]{2,1,0:T(8,128)}, f32[192,384]{1,0:T(8,128)}, bf16[256,1536]{1,0:T(8,128)(2,1)}) custom-call(bf16[256,3072]{1,0:T(8,128)(2,1)} %bitcast.5, bf16[256,3072]{1,0:T(8,128)(2,1)} %bitcast.6, bf16[3,192,384]{2,1,0:T(8,128)(2,1)} %bitcast.9, bf16[192,384]{1,0:T(8,128)(2,1)} %outw_hbm.1), custom_call_target="tpu_custom_call" | custom-call | tf_op jit(solution)/shard_map/layer/pallas_call | solution.py:1026
  139.7 0.0 copy-start.1
  139.7 0.0 copy-start
  139.7 2.2 %copy.10 = f32[192,3,384]{2,0,1:T(8,128)} copy(f32[192,3,384]{2,0,1:T(8,128)} %bitcast.7) | data formatting | bytes 1769472
  141.9 0.0 copy-done.1
  141.9 0.7 copy.11
  142.6 0.0 copy-done
  142.6 0.9 copy.12
Async XLA Ops:
  139.7 2.2 %copy-start.1 = (f32[192,384]{1,0:T(8,128)S(1)}, f32[192,384]{1,0:T(8,128)}, u32[]{:S(2)}) copy-start(f32[192,384]{1,0:T(8,128)} %get-tuple-element.13) | copy-start | bytes 884740
  139.7 3.0 %copy-start = (bf16[256,1536]{1,0:T(8,128)(2,1)S(1)}, bf16[256,1536]{1,0:T(8,128)(2,1)}, u32[]{:S(2)}) copy-start(bf16[256,1536]{1,0:T(8,128)(2,1)} %get-tuple-element.8) | copy-start | bytes 2359300

commit v4 on v3

--- a/solution.py
+++ b/solution.py
@@ -17,23 +17,38 @@
 (
     W_KV,
     OWN_QUERY,
+    OWN_OUT,
     SPREAD_QUERY,
+    SPREAD_OUT,
     CHIP_KV,
     MIX_KV,
     KEY_READY,
-    W_QO,
+    W_QUERY,
+    W_OUT,
     SEND_PAIRS,
     FLIP_UNIT,
     FLIP_COT,
-    CHIP_QO,
-    MIX_QO,
+    CHIP_QUERY,
+    CHIP_OUT,
+    MIX_QUERY,
+    MIX_OUT,
     PAIR,
     QUERY_READY,
+    LEND_QUERY,
     ATTEND,
     ATTEND_END,
+    BORROW_QUERY,
+    ATTEND_OTHER,
+    GIVE_OUT,
+    GRAD_READY,
+    LEND_GRAD,
     BACKWARD,
+    TAKE_OUT,
+    BORROW_GRAD,
+    BACKWARD_OTHER,
     FIRST_KEY,
     FIRST_VALUE,
+    GIVE_QUERY,
     MAKE_OUT,
     ACROSS_OUT,
     BACK_QUERY,
@@ -63,58 +78,73 @@
     FINISH_KEY,
     FINISH_BRANCH,
     FINISH_VALUE,
-) = range(48)
+) = range(63)
 FORWARD_TIMES = {
-    W_KV: (-4.87, 5.57),
-    OWN_QUERY: (-12.55, 3.56),
-    SPREAD_QUERY: (27.94, 1.11),
-    CHIP_KV: (11.34, 3.56),
-    MIX_KV: (29.29, 1.26),
-    KEY_READY: (20.32, 0.0),
-    W_QO: (26.16, 3.27),
-    SEND_PAIRS: (26.3, 0.47),
-    FLIP_UNIT: (52.59, 0.0),
-    FLIP_COT: (19.92, 1.65),
-    CHIP_QO: (37.05, 3.63),
-    MIX_QO: (34.13, 6.34),
-    PAIR: (42.23, 6.16),
-    QUERY_READY: (67.43, 6.51),
-    ATTEND: (45.34, 0.0),
-    ATTEND_END: (77.44, 0.0),
+    W_KV: (0.41, 2.48),
+    OWN_QUERY: (-35.12, 0.16),
+    OWN_OUT: (-28.38, 1.52),
+    SPREAD_QUERY: (7.47, 0.92),
+    SPREAD_OUT: (-12.93, 0.0),
+    CHIP_KV: (8.55, 3.24),
+    MIX_KV: (-32.56, 4.81),
+    KEY_READY: (5.33, 0.0),
+    W_QUERY: (22.56, 4.24),
+    W_OUT: (29.16, 3.65),
+    SEND_PAIRS: (34.01, 2.08),
+    FLIP_UNIT: (47.59, 3.24),
+    FLIP_COT: (-1.26, 5.59),
+    CHIP_QUERY: (36.68, 3.45),
+    CHIP_OUT: (51.83, 3.22),
+    MIX_QUERY: (53.59, 0.0),
+    MIX_OUT: (78.74, 2.36),
+    PAIR: (44.44, 1.99),
+    QUERY_READY: (27.52, 0.84),
+    LEND_QUERY: (8.55, 2.18),
+    ATTEND: (-3.33, 3.06),
+    ATTEND_END: (65.5, 0.0),
+    BORROW_QUERY: (53.42, 0.97),
+    ATTEND_OTHER: (33.53, 2.02),
+    GIVE_OUT: (31.15, 0.3),
+    GRAD_READY: (60.02, 0.25),
+    LEND_GRAD: (28.36, 0.0),
 }
 BACKWARD_TIMES = {
-    BACKWARD: (-2.19, 2.64),
-    FIRST_KEY: (-2.46, 1.91),
-    FIRST_VALUE: (6.2, 0.54),
-    MAKE_OUT: (1.52, 0.0),
-    ACROSS_OUT: (4.71, 0.17),
-    BACK_QUERY: (2.54, 0.0),
-    MAKE_QUERY: (-18.11, 0.64),
-    ACROSS_QUERY: (15.9, 0.82),
-    Y_OUT: (18.34, 0.0),
-    G_KEY: (3.85, 0.0),
-    OWN_KEY: (18.05, 1.39),
-    BACK_KEYS: (29.33, 0.5),
-    MAKE_KEY: (2.07, 0.03),
-    ACROSS_KEY: (9.4, 2.81),
-    G_VALUE: (21.95, 2.42),
-    OWN_VALUE: (32.26, 0.0),
-    BACK_VALUES: (47.91, 1.68),
-    MAKE_VALUE: (15.23, 0.0),
-    ACROSS_VALUE: (45.49, 1.78),
-    Y_QUERY: (38.62, 4.26),
-    Z_OUT: (30.05, 5.94),
-    INNER_GRAD: (52.42, 4.91),
-    Y_KEY: (46.6, 6.84),
-    Z_QUERY: (51.97, 0.56),
-    Y_VALUE: (59.28, 0.83),
-    Z_KEY: (53.48, 2.55),
-    Z_VALUE: (65.73, 6.14),
-    FINISH_OUT: (83.86, 0.52),
-    FINISH_QUERY: (68.47, 0.33),
-    FINISH_KEY: (78.69, 2.43),
-    FINISH_BRANCH: (89.16, 1.92),
-    FINISH_VALUE: (92.27, 0.0),
+    BACKWARD: (2.44, 0.88),
+    TAKE_OUT: (-26.82, 0.0),
+    BORROW_GRAD: (-12.76, 4.8),
+    BACKWARD_OTHER: (-3.78, 1.86),
+    FIRST_KEY: (-1.37, 1.7),
+    FIRST_VALUE: (10.84, 4.04),
+    GIVE_QUERY: (13.49, 1.36),
+    MAKE_OUT: (-43.71, 2.7),
+    ACROSS_OUT: (-1.45, 1.38),
+    BACK_QUERY: (-0.89, 0.0),
+    MAKE_QUERY: (8.55, 2.05),
+    ACROSS_QUERY: (1.13, 0.0),
+    Y_OUT: (10.77, 1.73),
+    G_KEY: (13.06, 4.75),
+    OWN_KEY: (-5.55, 0.0),
+    BACK_KEYS: (25.83, 0.21),
+    MAKE_KEY: (-0.38, 0.03),
+    ACROSS_KEY: (23.41, 0.74),
+    G_VALUE: (-2.95, 1.82),
+    OWN_VALUE: (26.8, 0.0),
+    BACK_VALUES: (9.31, 2.34),
+    MAKE_VALUE: (31.42, 4.75),
+    ACROSS_VALUE: (41.03, 0.54),
+    Y_QUERY: (18.18, 7.26),
+    Z_OUT: (27.24, 6.05),
+    INNER_GRAD: (33.2, 0.0),
+    Y_KEY: (39.48, 2.63),
+    Z_QUERY: (29.97, 5.88),
+    Y_VALUE: (50.93, 0.0),
+    Z_KEY: (35.92, 6.83),
+    Z_VALUE: (49.24, 5.92),
+    FINISH_OUT: (40.19, 1.65),
+    FINISH_QUERY: (51.68, 1.46),
+    FINISH_KEY: (70.55, 1.91),
+    FINISH_BRANCH: (78.24, 3.0),
+    FINISH_VALUE: (123.85, 3.1),
 }
 
 
@@ -122,7 +152,7 @@
     (BACK_KEYS, MAKE_KEY, ACROSS_KEY, Y_KEY, Z_KEY, FINISH_KEY),
     (BACK_VALUES, MAKE_VALUE, ACROSS_VALUE, Y_VALUE, Z_VALUE, FINISH_VALUE),
     (BACK_QUERY, MAKE_QUERY, ACROSS_QUERY, Y_QUERY, Z_QUERY, FINISH_QUERY),
-    (None, MAKE_OUT, ACROSS_OUT, Y_OUT, Z_OUT, FINISH_OUT),
+    (TAKE_OUT, MAKE_OUT, ACROSS_OUT, Y_OUT, Z_OUT, FINISH_OUT),
 )
 
 
@@ -131,36 +161,47 @@
 
 
 def forward_steps(seq_count):
-    events = 2 * (seq_count - 1)
-    needs = {(OWN_QUERY, 0): [(W_KV, min(4, events) - 1)] if events else [], (SPREAD_QUERY, 0): []}
-    for come, across, mix in ((W_KV, CHIP_KV, MIX_KV), (W_QO, CHIP_QO, MIX_QO)):
-        for n in range(events):
-            needs[come, n] = [(come, n - 1)] if n else []
-        for n in range(events + 2):
-            needs[across, n] = [(across, n - 1)] if n else []
-            if n > 1:
-                needs[across, n].append((come, n - 2))
-        for k in range(seq_count):
-            needs[mix, k] = [(across, 1 + events_until(k, seq_count))]
-            if k:
-                needs[mix, k].append((mix, k - 1))
-    for n in range(2):
-        needs[CHIP_QO, n].append((SPREAD_QUERY, 0))
-    if events:
-        needs[W_QO, 0] = [(OWN_QUERY, 1)]
-    needs[OWN_QUERY, 1] = [(OWN_QUERY, 0)] + ([(W_KV, events - 1)] if events else [])
+    events, needs = 2 * (seq_count - 1), {}
+
+    def chained(name, count, more):
+        for n in range(count):
+            needs[name, n] = ([(name, n - 1)] if n else []) + more(n)
+
+    chained(W_KV, events, lambda n: [])
+    chained(CHIP_KV, events + 2, lambda n: [(W_KV, n - 2)] if n > 1 else [])
+    chained(MIX_KV, seq_count, lambda k: [(CHIP_KV, 1 + events_until(k, seq_count))])
+    streams = (
+        (OWN_QUERY, SPREAD_QUERY, W_QUERY, CHIP_QUERY, MIX_QUERY),
+        (OWN_OUT, SPREAD_OUT, W_OUT, CHIP_OUT, MIX_OUT),
+    )
+    for own, spread, come, across, mix in streams:
+        needs[own, 0] = [(W_KV, min(4, events) - 1)]
+        needs[own, 1] = [(own, 0), (W_KV, events - 1)]
+        needs[spread, 0] = [(own, 1)]
+        chained(come, seq_count - 1, lambda n: [(own, 1)])
+        chained(across, seq_count, lambda n: [(come, n - 1)] if n else [(spread, 0)])
+        chained(mix, seq_count, lambda n: [(across, n)])
+    needs[W_OUT, 0].append((W_QUERY, seq_count - 2))
+    needs[SPREAD_OUT, 0].append((W_QUERY, seq_count - 2))
+    needs[CHIP_OUT, 0].append((CHIP_QUERY, seq_count - 1))
     needs[KEY_READY, 0] = [(MIX_KV, seq_count - 1)]
     needs[SEND_PAIRS, 0] = [(KEY_READY, 0)]
     needs[FLIP_UNIT, 0] = needs[FLIP_COT, 0] = []
-    for n in range(events):
-        needs[PAIR, n] = [(PAIR, n - 1) if n else (SEND_PAIRS, 0)]
-    needs[QUERY_READY, 0] = [(MIX_QO, seq_count - 1)]
-    for k in range(seq_count):
-        needs[ATTEND, k] = [(ATTEND, k - 1) if k else (QUERY_READY, 0), (KEY_READY, 0)]
-        if events_until(k, seq_count):
-            needs[ATTEND, k].append((PAIR, events_until(k, seq_count) - 1))
-    ends = [(ATTEND, seq_count - 1), (FLIP_UNIT, 0), (FLIP_COT, 0)]
-    needs[ATTEND_END, 0] = ends
+    chained(PAIR, events, lambda n: [(SEND_PAIRS, 0)])
+    needs[QUERY_READY, 0] = [(MIX_QUERY, seq_count - 1)]
+    needs[LEND_QUERY, 0] = [(QUERY_READY, 0)]
+    needs[BORROW_QUERY, 0] = [(LEND_QUERY, 0)]
+
+    def there(k):
+        until = events_until(k, seq_count)
+        return [(KEY_READY, 0)] + ([(PAIR, until - 1)] if until else [])
+
+    chained(ATTEND, seq_count, lambda k: [(QUERY_READY, 0)] + there(k))
+    chained(ATTEND_OTHER, seq_count, lambda k: [(BORROW_QUERY, 0)] + there(k))
+    needs[ATTEND_END, 0] = [(ATTEND, seq_count - 1)]
+    needs[GIVE_OUT, 0] = [(ATTEND_OTHER, seq_count - 1)]
+    needs[GRAD_READY, 0] = [(MIX_OUT, seq_count - 1)]
+    needs[LEND_GRAD, 0] = [(GRAD_READY, 0)]
     return in_order(needs, FORWARD_TIMES)
 
 
@@ -173,14 +214,17 @@
 
     chained(BACKWARD, seq_count, lambda n: [])
     for first, come, own in ((FIRST_KEY, G_KEY, OWN_KEY), (FIRST_VALUE, G_VALUE, OWN_VALUE)):
-        chained(first, seq_count, lambda n: [(BACKWARD, n)])
+        chained(first, seq_count, lambda n: [(BACKWARD_OTHER, n)])
         chained(come, last, lambda n: [(first, last)])
         needs[own, 0] = [(come, last - 1) if last else (first, last)]
-    needs[BACK_QUERY, 0] = [(BACKWARD, last)]
+    needs[BORROW_GRAD, 0] = needs[TAKE_OUT, 0] = []
+    chained(BACKWARD_OTHER, seq_count, lambda n: [(BACKWARD, n), (BORROW_GRAD, 0)])
+    needs[GIVE_QUERY, 0] = [(BACKWARD_OTHER, last)]
+    needs[BACK_QUERY, 0] = [(BACKWARD, last), (GIVE_QUERY, 0)]
     needs[BACK_KEYS, 0] = [(OWN_KEY, 0)]
     needs[BACK_VALUES, 0] = [(OWN_VALUE, 0)]
     for ready, make, across, come, chain, finish in PIECES:
-        first = [] if ready is None else [(ready, 0)]
+        first = [(ready, 0)]
         chained(make, seq_count, lambda n: first)
         chained(across, seq_count, lambda n: [(make, n)])
         chained(come, seq_count, lambda n: [(across, n)])
@@ -250,6 +294,8 @@
     query_inv,
     key_inv,
     grad_low,
+    query_out,
+    query_in,
     expo,
     totals,
     deltas,
@@ -280,6 +326,8 @@
     g_low,
     g_high,
     g_send,
+    h_send,
+    h_recv,
     t_core_recv,
     t_chip_recv,
     t_send,
@@ -302,6 +350,10 @@
     chip, core = index // CORES, index % CORES
     not_last, not_first = place < seq_count - 1, place > 0
     both_sides = jnp.minimum(place, seq_count - 1 - place)
+    at_end = both_sides == 0
+    inside = both_sides > 0
+    helps = both_sides == 1
+    can_right, can_left = place < seq_count - 2, place > 1
     KEY, VALUE, QUERY, OUT = range(4)
 
     def rows_of(slot):
@@ -380,46 +432,40 @@
             piece, k = rest % 2, 2 * group + 1 + rest // 2
         return piece, origin_at(k)
 
-    def w_copy(piece, slot, send_sem, device):
+    def w_copy(piece, slot, send_sem, device, source=None):
         ref = weights.at[piece, rows_of(slot), :]
-        return remote(ref, ref, send_sem, w_recv.at[piece, slot], device)
-
-    def w_side(piece, origin, rightward):
+        return remote(ref if source is None else source, ref, send_sem, w_recv.at[piece, slot], device)
+
+    def w_side(piece, origin, rightward, source=None):
         if rightward:
-            return w_copy(piece, origin * dp_count + index, w_send.at[0], up)
-        return w_copy(piece, origin * dp_count + index, w_send.at[0], down)
-
-    def w_across(piece, origin, step):
-        return w_copy(piece, origin * dp_count + index, w_send.at[1], chip_device(step))
-
-    def w_beside(piece, origin, source_chip):
+            return w_copy(piece, origin * dp_count + index, w_send.at[0], up, source)
+        return w_copy(piece, origin * dp_count + index, w_send.at[0], down, source)
+
+    def w_across(piece, origin, step, source=None):
+        return w_copy(piece, origin * dp_count + index, w_send.at[1], chip_device(step), source)
+
+    def w_beside(piece, origin, source_chip, source=None):
         slot = origin * dp_count + source_chip * CORES + core
-        return w_copy(piece, slot, w_send.at[2], beside_device)
+        return w_copy(piece, slot, w_send.at[2], beside_device, source)
 
     def w_landed(piece, slot):
         w_copy(piece, slot, w_send.at[2], beside_device).wait_recv()
 
-    def w_sides_own(first):
-        for piece in (first, first + 1):
-
-            @pl.when(not_last)
-            def _():
-                w_side(piece, place, True).start()
-
-            @pl.when(not_first)
-            def _():
-                w_side(piece, place, False).start()
-
-    def w_spread_own(first):
-        for piece in (first, first + 1):
-            for step in range(1, chip_count):
-                w_across(piece, place, step).start()
-        for piece in (first, first + 1):
-            w_beside(piece, place, chip).start()
-
-    def w_step(first, number):
-        piece, origin = event(number)
-        piece = piece + first
+    def w_sides_own(piece, source=None):
+        @pl.when(not_last)
+        def _():
+            w_side(piece, place, True, source).start()
+
+        @pl.when(not_first)
+        def _():
+            w_side(piece, place, False, source).start()
+
+    def w_spread_own(piece, source=None):
+        for step in range(1, chip_count):
+            w_across(piece, place, step, source).start()
+        w_beside(piece, place, chip, source).start()
+
+    def w_step(piece, origin):
         w_landed(piece, origin * dp_count + index)
 
         @pl.when((origin < place) & not_last)
@@ -434,27 +480,23 @@
             w_across(piece, origin, step).start()
         w_beside(piece, origin, chip).start()
 
-    def w_chip_step(first, number):
-        piece, origin = (number, place) if number < 2 else event(number - 2)
-        piece = piece + first
+    def w_chip_step(piece, origin):
         for step in range(1, chip_count):
             source_chip = (chip + step) % chip_count
             w_landed(piece, origin * dp_count + source_chip * CORES + core)
             w_beside(piece, origin, source_chip).start()
 
-    def project(first, k):
+    def project(piece, k):
         origin = origin_at(k)
         rows = pl.ds(pl.multiple_of(origin * plane, plane), plane)
-        for piece in (first, first + 1):
-            for source_chip in range(chip_count):
-                w_landed(piece, origin * dp_count + source_chip * CORES + 1 - core)
-        for piece in (first, first + 1):
-            source = cot if piece == OUT else unit_low
-            product = dot(source[:, rows], weights[piece, rows, :])
-            if k == 0:
-                acc[piece] = product
-            else:
-                acc[piece] += product
+        for source_chip in range(chip_count):
+            w_landed(piece, origin * dp_count + source_chip * CORES + 1 - core)
+        source = cot if piece == OUT else unit_low
+        product = dot(source[:, rows], weights[piece, rows, :])
+        if k == 0:
+            acc[piece] = product
+        else:
+            acc[piece] += product
 
     def p_copy(piece, origin, rightward):
         ref = pairs.at[piece, block_rows(origin), :]
@@ -464,26 +506,62 @@
 
     def p_step(number):
         piece, origin = event(number)
-        p_copy(piece, origin, True).wait_recv()
-
-        @pl.when((origin < place) & not_last)
-        def _():
-            p_copy(piece, origin, True).start()
-
-        @pl.when((origin > place) & not_first)
-        def _():
-            p_copy(piece, origin, False).start()
+
+        @pl.when(inside)
+        def _():
+            p_copy(piece, origin, True).wait_recv()
+
+            @pl.when((origin < place) & can_right)
+            def _():
+                p_copy(piece, origin, True).start()
+
+            @pl.when((origin > place) & can_left)
+            def _():
+                p_copy(piece, origin, False).start()
 
     def p_sides_own():
         for piece in range(2):
 
-            @pl.when(not_last)
+            @pl.when(can_right)
             def _():
                 p_copy(piece, place, True).start()
 
-            @pl.when(not_first)
+            @pl.when(can_left)
             def _():
                 p_copy(piece, place, False).start()
+
+    def loan(source, target, number, device):
+        return remote(source, target, h_send.at[number], h_recv.at[number], device)
+
+    def lend(source, target, number):
+        @pl.when(place == 0)
+        def _():
+            loan(source, target, number, up).start()
+
+        @pl.when(place == seq_count - 1)
+        def _():
+            loan(source, target, number, down).start()
+
+    def give(source, target, number):
+        @pl.when(place == 1)
+        def _():
+            loan(source, target, number, down).start()
+
+        @pl.when(place == seq_count - 2)
+        def _():
+            loan(source, target, number, up).start()
+
+    def loans():
+        return (
+            (query_low.at[0], query_low.at[1]),
+            (grad_low.at[0], grad_low.at[1]),
+            (attended.at[1], attended.at[0]),
+            (query_out, query_in),
+        )
+
+    def loan_wait(number):
+        source, target = loans()[number]
+        loan(source, target, number, up).wait_recv()
 
     def normalize_tokens():
         @pl.loop(0, token_count // 32)
@@ -519,82 +597,119 @@
             normed, inverse = normalize(acc[QUERY, :, cut])
             query_unit[:, cut] = normed
             query_inv[:, cut] = jnp.broadcast_to(inverse, (token_count, HD))
-            query_low[:, cut] = normed.astype(BF16)
-        grad_low[...] = acc[OUT].astype(BF16)
-
-    loads[0].wait()
-    w_sides_own(KEY)
-    w_spread_own(KEY)
-    for load in loads[1:]:
+            query_low[0, :, cut] = normed.astype(BF16)
+
+    def grad_ready():
+        grad_low[0] = acc[OUT].astype(BF16)
+
+    for piece in (KEY, VALUE):
+        w_sides_own(piece, qkv_hbm.at[1 + piece])
+    for piece in (KEY, VALUE):
+        w_spread_own(piece, qkv_hbm.at[1 + piece])
+    for load in loads:
         load.wait()
     normalize_tokens()
 
-    def head_cut(h):
-        return pl.ds(pl.multiple_of(h * HD, HD), HD)
-
-    def expo_at(origin, h):
-        row = (h * seq_count + origin) * token_count
+    def expo_at(who, origin, h):
+        row = ((who * head_count + h) * seq_count + origin) * token_count
         return pl.ds(pl.multiple_of(row, token_count), token_count)
 
-    def attend(k):
+    def attend_rows(who, k):
         origin = origin_at(k)
-
-        @pl.loop(0, head_count)
-        def _(h):
-            cut = head_cut(h)
-            rows = block_rows(origin)
-            scores = dot_nt(query_low[:, cut], pairs[0, rows, cut]) * scale
+        rows = block_rows(origin)
+        for h in range(head_count):
+            cut = slice(h * HD, (h + 1) * HD)
+            scores = dot_nt(query_low[who, :, cut], pairs[0, rows, cut]) * scale
             exponent = jnp.exp(scores)
             low = exponent.astype(BF16)
-            expo[expo_at(origin, h), :] = low
+            expo[expo_at(who, origin, h), :] = low
             total = exponent[:, :HD]
             for at in range(HD, token_count, HD):
                 total = total + exponent[:, at : at + HD]
             mixed = dot(low, pairs[1, rows, cut])
             if k == 0:
-                totals[h] = total
-                weighted[:, cut] = mixed
+                totals[who * head_count + h] = total
+                weighted[who, :, cut] = mixed
             else:
-                totals[h] += total
-                weighted[:, cut] += mixed
-
-    def attend_end():
+                totals[who * head_count + h] += total
+                weighted[who, :, cut] += mixed
+
+    def attend(k):
+        pl.when(inside)(lambda: attend_rows(0, k))
+
+    def attend_other(k):
+        pl.when(helps)(lambda: attend_rows(1, k))
+
+    def attend_end(who):
         for h in range(head_count):
             cut = slice(h * HD, (h + 1) * HD)
-            total = jnp.sum(totals[h], axis=-1, keepdims=True)
-            low = (weighted[:, cut] / total).astype(BF16)
-            attended[:, cut] = low
-            both = grad_low[:, cut].astype(F32) * low.astype(F32)
-            totals[h] = jnp.broadcast_to(1.0 / total, (token_count, HD))
-            deltas[h] = jnp.broadcast_to(jnp.sum(both, axis=-1, keepdims=True), (token_count, HD))
-
-    at_end = both_sides == 0
-
-    def own_query(number):
-        @pl.when(jnp.logical_not(at_end) if number else at_end)
-        def _():
-            w_sides_own(QUERY)
+            total = jnp.sum(totals[who * head_count + h], axis=-1, keepdims=True)
+            attended[who, :, cut] = (weighted[who, :, cut] / total).astype(BF16)
+            totals[who * head_count + h] = jnp.broadcast_to(1.0 / total, (token_count, HD))
+
+    def attend_delta(who):
+        for h in range(head_count):
+            cut = slice(h * HD, (h + 1) * HD)
+            both = grad_low[who, :, cut].astype(F32) * attended[who, :, cut].astype(F32)
+            delta = jnp.sum(both, axis=-1, keepdims=True)
+            deltas[who * head_count + h] = jnp.broadcast_to(delta, (token_count, HD))
+
+    def own_stream(piece, number):
+        @pl.when(inside if number else at_end)
+        def _():
+            w_sides_own(piece)
+
+    def kv_step(number):
+        piece, origin = event(number)
+        w_step(piece, origin)
+
+    def kv_chip(number):
+        piece, origin = (number, place) if number < 2 else event(number - 2)
+        w_chip_step(piece, origin)
+
+    def kv_mix(k):
+        project(KEY, k)
+        project(VALUE, k)
+
+    def give_out():
+        @pl.when(helps)
+        def _():
+            attend_end(1)
+            give(*loans()[2], 2)
 
     ahead = {
-        W_KV: lambda n: w_step(KEY, n),
-        OWN_QUERY: own_query,
+        W_KV: kv_step,
+        OWN_QUERY: lambda n: own_stream(QUERY, n),
+        OWN_OUT: lambda n: own_stream(OUT, n),
         SPREAD_QUERY: lambda n: w_spread_own(QUERY),
-        CHIP_KV: lambda n: w_chip_step(KEY, n),
-        MIX_KV: lambda n: project(KEY, n),
+        SPREAD_OUT: lambda n: w_spread_own(OUT),
+        CHIP_KV: kv_chip,
+        MIX_KV: kv_mix,
         KEY_READY: lambda n: key_ready(),
-        W_QO: lambda n: w_step(QUERY, n),
+        W_QUERY: lambda n: w_step(QUERY, origin_at(n + 1)),
+        W_OUT: lambda n: w_step(OUT, origin_at(n + 1)),
+        CHIP_QUERY: lambda n: w_chip_step(QUERY, origin_at(n)),
+        CHIP_OUT: lambda n: w_chip_step(OUT, origin_at(n)),
+        MIX_QUERY: lambda n: project(QUERY, n),
+        MIX_OUT: lambda n: project(OUT, n),
         SEND_PAIRS: lambda n: p_sides_own(),
         FLIP_UNIT: lambda n: flip(unit_low, unit_t),
         FLIP_COT: lambda n: flip(cot, cot_t),
-        CHIP_QO: lambda n: w_chip_step(QUERY, n),
-        MIX_QO: lambda n: project(QUERY, n),
         PAIR: p_step,
         QUERY_READY: lambda n: query_ready(),
+        LEND_QUERY: lambda n: lend(*loans()[0], 0),
+        BORROW_QUERY: lambda n: pl.when(helps)(lambda: loan_wait(0)),
         ATTEND: attend,
-        ATTEND_END: lambda n: attend_end(),
+        ATTEND_OTHER: attend_other,
+        ATTEND_END: lambda n: pl.when(inside)(lambda: attend_end(0)),
+        GIVE_OUT: lambda n: give_out(),
+        GRAD_READY: lambda n: grad_ready(),
+        LEND_GRAD: lambda n: lend(*loans()[1], 1),
     }
     for name, number in forward_steps(seq_count):
         ahead[name](number)
+
+    pl.when(inside)(lambda: attend_delta(0))
 
     def target_at(n):
         return origin_at(seq_count - 1 - n)
@@ -623,67 +738,100 @@
         into = part_in.at[piece, into, :]
         return remote(source, into, g_send.at[0], sem.at[piece, target], device)
 
+    def backward_rows(who, n):
+        target = target_at(n)
+        rows = block_rows(target)
+        for h in range(head_count):
+            cut = slice(h * HD, (h + 1) * HD)
+            inv_total = totals[who * head_count + h][:, :1]
+            probability = expo[expo_at(who, target, h), :].astype(F32) * inv_total
+            gradient = grad_low[who, :, cut]
+            prob_grad = dot_nt(gradient, pairs[1, rows, cut])
+            delta = deltas[who * head_count + h][:, :1]
+            score = (probability * (prob_grad - delta) * scale).astype(BF16)
+            query_part = dot(score, pairs[0, rows, cut])
+            key_part = dot_tn(score, query_low[who, :, cut])
+            value_part = dot_tn(probability.astype(BF16), gradient)
+            if who:
+                key_part = key_part + part[0, rows, cut].astype(F32)
+                value_part = value_part + part[1, rows, cut].astype(F32)
+            part[0, rows, cut] = key_part.astype(BF16)
+            part[1, rows, cut] = value_part.astype(BF16)
+            if n == 0:
+                query_raw[who, :, cut] = query_part
+            else:
+                query_raw[who, :, cut] += query_part
+
     def backward(n):
-        target = target_at(n)
-
-        @pl.loop(0, head_count)
-        def _(h):
-            cut = head_cut(h)
-            rows = block_rows(target)
-            inv_total = totals[h][:, :1]
-            probability = expo[expo_at(target, h), :].astype(F32) * inv_total
-            gradient = grad_low[:, cut]
-            prob_grad = dot_nt(gradient, pairs[1, rows, cut])
-            score = (probability * (prob_grad - deltas[h][:, :1]) * scale).astype(BF16)
-            query_part = dot(score, pairs[0, rows, cut])
-            part[0, rows, cut] = dot_tn(score, query_low[:, cut]).astype(BF16)
-            part[1, rows, cut] = dot_tn(probability.astype(BF16), gradient).astype(BF16)
-            if n == 0:
-                query_raw[:, cut] = query_part
-            else:
-                query_raw[:, cut] += query_part
+        pl.when(inside)(lambda: backward_rows(0, n))
+
+    def backward_other(n):
+        pl.when(helps)(lambda: backward_rows(1, n))
+
+    def borrow_grad():
+        @pl.when(helps)
+        def _():
+            loan_wait(1)
+            attend_delta(1)
+
+    def give_query():
+        @pl.when(helps)
+        def _():
+            query_out[...] = query_raw[1].astype(BF16)
+            give(*loans()[3], 3)
 
     def g_first(piece, n):
         target = target_at(n)
 
-        @pl.when((target > place) & (place == 0))
+        @pl.when((target > place) & (place == 1))
         def _():
             g_copy(piece, target, True).start()
 
-        @pl.when((target < place) & (place == seq_count - 1))
+        @pl.when((target < place) & (place == seq_count - 2))
         def _():
             g_copy(piece, target, False).start()
 
     def g_step(piece, n):
         target = target_at(n)
 
-        @pl.when((place < target) & not_first)
+        @pl.when((place < target) & inside & can_left)
         def _():
             g_copy(piece, target, True).wait_recv()
             add_into(part, piece, target, [(part_in, target)], token_count)
             g_copy(piece, target, True).start()
 
-        @pl.when((place > target) & not_last)
+        @pl.when((place > target) & inside & can_right)
         def _():
             g_copy(piece, target, False).wait_recv()
             add_into(part, piece, target, [(part_in, target)], token_count)
             g_copy(piece, target, False).start()
 
     def g_own(piece):
-        @pl.when(not_first)
+        own = block_rows(place)
+
+        @pl.when(at_end)
+        def _():
+            part[piece, own, :] = jnp.zeros((token_count, head_count * HD), BF16)
+
+        @pl.when(can_left)
         def _():
             g_copy(piece, place, True).wait_recv()
             add_into(part, piece, place, [(part_in, place)], token_count)
 
-        @pl.when(not_last)
+        @pl.when(can_right)
         def _():
             g_copy(piece, place, False).wait_recv()
             add_into(part, piece, place, [(part_in, seq_count)], token_count)
 
     def back_query():
+        @pl.when(at_end)
+        def _():
+            loan_wait(3)
+            query_raw[0] = query_in[...].astype(F32)
+
         for h in range(head_count):
             cut = slice(h * HD, (h + 1) * HD)
-            raised = normalize_back(query_raw[:, cut], query_unit[:, cut], query_inv[:, cut])
+            raised = normalize_back(query_raw[0, :, cut], query_unit[:, cut], query_inv[:, cut])
             back[QUERY, :, cut] = raised.astype(BF16)
 
     def back_keys():
@@ -725,7 +873,7 @@
         target = target_at(n)
         source = cot_t if piece == OUT else unit_t
 
-        right = attended[...] if piece == OUT else back[piece]
+        right = attended[0] if piece == OUT else back[piece]
         size = plane // CORES
         for at in range(CORES):
             rows = pl.ds(pl.multiple_of(target * plane + at * size, size), size)
@@ -891,6 +1039,10 @@
 
     behind = {
         BACKWARD: backward,
+        TAKE_OUT: lambda n: pl.when(at_end)(lambda: loan_wait(2)),
+        BORROW_GRAD: lambda n: borrow_grad(),
+        BACKWARD_OTHER: backward_other,
+        GIVE_QUERY: lambda n: give_query(),
         FIRST_KEY: lambda n: g_first(0, n),
         FIRST_VALUE: lambda n: g_first(1, n),
         BACK_QUERY: lambda n: back_query(),
@@ -928,16 +1080,27 @@
         left(held, both * own_rows, t_send.at[0])
         if seq_count > 1:
             left(chain_in, (seq_count - 1) * own_rows, t_send.at[2])
-            left(part, (seq_count - 1) * token_count, g_send.at[0])
 
             @pl.when(at_end)
             def _():
                 left(weights, own_rows, w_send.at[0])
                 left(part_in, token_count, p_send.at[0])
-
-            @pl.when(jnp.logical_not(at_end))
+                for number in (0, 1):
+                    loan(*loans()[number], number, up).wait_send()
+
+            @pl.when(inside)
             def _():
                 left(weights, (seq_count + 1) * own_rows, w_send.at[0])
+                left(part, (seq_count - 1) * token_count, g_send.at[0])
+
+            @pl.when(helps)
+            def _():
+                left(part_in, 2 * token_count, p_send.at[0])
+                for number in (2, 3):
+                    loan(*loans()[number], number, up).wait_send()
+
+            @pl.when(both_sides > 1)
+            def _():
                 left(part_in, (seq_count + 1) * token_count, p_send.at[0])
 
         for step in range(1, tensor_count):
@@ -955,6 +1118,7 @@
     own_rows, columns = out_weight.shape
     head_count = columns // HD
     share = feature_count // tensor_count
+    assert seq_count > 3
     sizes = (seq_count, dp_count, tensor_count, own_rows, head_count)
 
     def vmem(*shape, kind=BF16):
@@ -976,18 +1140,20 @@
         vmem(4, feature_count, columns),
         vmem(4, row_count, columns, kind=F32),
         vmem(2, seq_count * row_count, columns),
-        vmem(row_count, columns),
+        vmem(2, row_count, columns),
         vmem(row_count, columns, kind=F32),
         vmem(row_count, columns, kind=F32),
         vmem(row_count, columns, kind=F32),
         vmem(row_count, columns, kind=F32),
+        vmem(2, row_count, columns),
         vmem(row_count, columns),
-        vmem(head_count * seq_count * row_count, row_count),
-        vmem(head_count, row_count, HD, kind=F32),
-        vmem(head_count, row_count, HD, kind=F32),
-        vmem(row_count, columns, kind=F32),
         vmem(row_count, columns),
-        vmem(row_count, columns, kind=F32),
+        vmem(2 * head_count * seq_count * row_count, row_count),
+        vmem(2 * head_count, row_count, HD, kind=F32),
+        vmem(2 * head_count, row_count, HD, kind=F32),
+        vmem(2, row_count, columns, kind=F32),
+        vmem(2, row_count, columns),
+        vmem(2, row_count, columns, kind=F32),
         vmem(2, seq_count * row_count, columns),
         vmem(2, (seq_count + 1) * row_count, columns),
         vmem(3, row_count, columns),
@@ -1012,6 +1178,8 @@
         dma(2, seq_count),
         dma(2, seq_count),
         dma(1),
+        dma(4),
+        dma(4),
         dma(4, both),
         dma(4, peers),
         dma(3),

time: 144 us -> 136 us (0.944)
  Pallas kernels: 139 us -> 131 us
    pallas_call x1, Pallas kernels: 139 us -> 131 us  [local(): pl.pallas_call(functools.partial(body, sizes), out_shape=(jax.ShapeDtypeS...]
where the time goes in v4:
time: 136 us; the launch traced here: 135 us
  Pallas kernels  131 us (96%)
  local copies, waits for them, and re-layouts  3.83 us (3%)
    pallas_call x1, Pallas kernels, local(): pl.pallas_call(functools.partial(body, sizes), out_shape=(jax.ShapeDtypeS...  131 us
    unnamed x7, local copies, waits for them, and re-layouts  3.83 us

profile of v4, /device:TPU:0, one launch (start us, length us, event | category | flops | bytes accessed | tf_op | source)
XLA Modules:
  0.0 135.5 jit_solution(1888526692813036906)
XLA Ops:
  0.6 131.0 %layer.1 = (f32[3,192,384]{2,1,0:T(8,128)}, f32[192,384]{1,0:T(8,128)}, bf16[256,1536]{1,0:T(8,128)(2,1)}) custom-call(bf16[256,3072]{1,0:T(8,128)(2,1)} %bitcast.5, bf16[256,3072]{1,0:T(8,128)(2,1)} %bitcast.6, bf16[3,192,384]{2,1,0:T(8,128)(2,1)} %bitcast.9, bf16[192,384]{1,0:T(8,128)(2,1)} %outw_hbm.1), custom_call_target="tpu_custom_call" | custom-call | tf_op jit(solution)/shard_map/layer/pallas_call | solution.py:1194
  131.6 0.0 copy-start.1
  131.6 0.0 copy-start
  131.6 2.2 %copy.10 = f32[192,3,384]{2,0,1:T(8,128)} copy(f32[192,3,384]{2,0,1:T(8,128)} %bitcast.7) | data formatting | bytes 1769472
  133.9 0.0 copy-done.1
  133.9 0.7 copy.11
  134.6 0.0 copy-done
  134.6 0.9 copy.12
Async XLA Ops:
  131.6 2.2 %copy-start.1 = (f32[192,384]{1,0:T(8,128)S(1)}, f32[192,384]{1,0:T(8,128)}, u32[]{:S(2)}) copy-start(f32[192,384]{1,0:T(8,128)} %get-tuple-element.13) | copy-start | bytes 884740
  131.6 3.0 %copy-start = (bf16[256,1536]{1,0:T(8,128)(2,1)S(1)}, bf16[256,1536]{1,0:T(8,128)(2,1)}, u32[]{:S(2)}) copy-start(bf16[256,1536]{1,0:T(8,128)(2,1)} %get-tuple-element.8) | copy-start | bytes 2359300
